TPU v7x, 128 devices: a whole 4x4x4 slice. The times are simulated.
128 devices in a mesh: grp: 4 (over z), dev: 32 (over x, y, core).
Axes of the slice: x: 4, y: 4, z: 4, core: 2. Of those that a mesh axis runs over, the one named last changes fastest.
Arguments:
- qkv_weight: bfloat16 [2, 4608, 8192], P(None, ('grp', 'dev')), may hold values from -0.09375 to 0.09375
- gate_up_weight: bfloat16 [2, 4608, 73728], P(None, ('grp', 'dev')), may hold values from -0.09375 to 0.09375
- head_slot: int32 [64], replicated, may hold values from 0 to 63, each once
- layer_ids: int32 [2], replicated, may hold values from 0 to 45
- stored_qkv: int32 [46, 64], replicated, may hold values from -16384 to 16383
- stored_gate_up: int32 [46, 576], replicated, may hold values from -16384 to 16383
Outputs:
- served_qkv: bfloat16 [2, 4608, 8192], P(None, 'grp', 'dev')
- served_gate_up: bfloat16 [2, 4608, 73728], P(None, 'grp', 'dev')
- qkv_mismatch: float32 [2, 64], P(None, 'dev')
- gate_up_mismatch: float32 [2, 576], P(None, 'dev')
Inputs may be any that keep to these rules, and one draw needn't show every extreme that they name: `head_slot`: each of the 64 heads appears once.
All inputs are finite; a program needn't handle non-finite values.
Results may differ from a plain program's by a relative error of at most 0.0004.
Values may be sent and summed in bfloat16 or wider, within the bound.
No kernel may reach another device: no remote copies, remote signals or barrier semaphores. Data moves between devices by JAX's collectives and lax.ppermute only.
A program may use at most 128 MiB of HBM per device.

v0:
```python
import jax
import jax.numpy as jnp
from jax import lax
from jax.sharding import PartitionSpec as P

HEAD_DIM = 128
FF = 36864
STORED = 46
BLK = 128
NHEAD = 64


stored_unit = 1.0 / 1024.0


def cut_along(x, dim, length):
    dims = x.shape
    blocks = x.reshape(*dims[:dim], length, dims[dim] // length, *dims[dim + 1 :])
    return jnp.moveaxis(blocks, dim, 0)


def piece_ends(length, count):
    hop = length // count
    if hop >= 8:
        hop -= hop % 8
    return [hop * k for k in range(1, count)]


def in_order(blocks, dim):
    dims = list(blocks.shape[1:])
    dims[dim] *= blocks.shape[0]
    return jnp.moveaxis(blocks, 0, dim).reshape(dims)


def several_exchanges(x, axis, pieces, split_dim, concat_dim):
    blocks = cut_along(x, split_dim, lax.axis_size(axis))
    split_at = max(range(1, max(2, blocks.ndim - 1)), key=lambda d: blocks.shape[d])
    outs = []
    for piece in jnp.split(blocks, piece_ends(blocks.shape[split_at], pieces), axis=split_at):
        if piece.size:
            outs.append(lax.all_to_all(piece, axis, split_axis=0, concat_axis=0, tiled=True))
    return in_order(jnp.concatenate(outs, axis=split_at), concat_dim)


def copy_for_each(x, axis):
    copies = jnp.broadcast_to(x, (lax.axis_size(axis), *x.shape))
    return lax.all_to_all(copies, axis, split_axis=0, concat_axis=0, tiled=True)


def taken_together(x, axis):
    everything = copy_for_each(x, axis)
    return jnp.sum(everything, axis=0)


def packed_total(arrays, axis):
    ends = [0]
    for a in arrays:
        ends.append(ends[-1] + a.size)
    total = taken_together(jnp.concatenate([a.ravel() for a in arrays]), axis)
    return tuple((total[b:e].reshape(a.shape) for a, b, e in zip(arrays, ends, ends[1:])))


def finish(pieces):
    qkv_piece, gate_piece = pieces
    count = qkv_piece.shape[0]
    height = qkv_piece.shape[1]
    served_qkv = qkv_piece.reshape(count, height, qkv_piece.shape[4])
    served_gate = gate_piece.reshape(count, height, 2 * gate_piece.shape[4])
    head_local = jnp.sum(
        served_qkv.astype(jnp.float32).reshape(count, height, -1, HEAD_DIM), axis=(1, 3)
    )
    block_local = jnp.sum(
        served_gate.astype(jnp.float32).reshape(count, height, -1, BLK), axis=(1, 3)
    )
    return (served_qkv, served_gate, head_local, block_local)


def body(qkv_weight, gate_up_weight, head_slot, layer_ids, stored_qkv, stored_gate_up):
    owners = lax.axis_size("dev")
    owner = lax.axis_index("dev")
    layers = qkv_weight.shape[0]
    rows = qkv_weight.shape[1]
    slots = NHEAD // owners
    width = FF // owners
    blocks = width // BLK
    ordered = qkv_weight.reshape(layers, rows, NHEAD, HEAD_DIM)[:, :, head_slot, :]
    qkv_split = ordered.reshape(layers, rows, 1, owners, slots * HEAD_DIM)
    gate_split = gate_up_weight.reshape(layers, rows, 2, owners, width)
    moved = (
        several_exchanges(qkv_split, "dev", 2, 3, 1),
        several_exchanges(gate_split, "dev", 2, 3, 1),
    )
    results = finish(moved)
    served_qkv = results[0]
    served_gate = results[1]
    head_sum, block_sum = packed_total((results[2], results[3]), "grp")
    layer_pick = (layer_ids[:, None] == jnp.arange(STORED, dtype=jnp.int32)[None, :]).astype(
        jnp.float32
    )
    picked_qkv = jnp.dot(
        layer_pick,
        stored_qkv.astype(jnp.float32),
        precision=lax.Precision.HIGHEST,
        preferred_element_type=jnp.float32,
    )
    picked_gate = jnp.dot(
        layer_pick,
        stored_gate_up.astype(jnp.float32),
        precision=lax.Precision.HIGHEST,
        preferred_element_type=jnp.float32,
    )
    own_heads = lax.dynamic_slice_in_dim(head_slot, owner * slots, slots, 0)
    picked_qkv = picked_qkv[:, own_heads]
    picked_gate = (
        picked_gate.reshape(layers, 2, owners, blocks)
        .transpose(0, 2, 1, 3)
        .reshape(layers, owners * 2 * blocks)
    )
    picked_gate = lax.dynamic_slice_in_dim(picked_gate, owner * 2 * blocks, 2 * blocks, 1)
    qkv_mismatch = head_sum - picked_qkv * stored_unit
    gate_up_mismatch = block_sum - picked_gate * stored_unit
    return (served_qkv, served_gate, qkv_mismatch, gate_up_mismatch)


def solution(mesh):
    placed = (P(None, ("grp", "dev"), None), P(None, ("grp", "dev"), None), P(), P(), P(), P())
    return jax.shard_map(
        body,
        mesh=mesh,
        in_specs=placed,
        out_specs=(P(None, "grp", "dev"), P(None, "grp", "dev"), P(None, "dev"), P(None, "dev")),
        check_vma=False,
    )
```

profile of v0, /device:TPU:40, one launch (start us, length us, event | category | flops | bytes accessed | tf_op | source)
XLA Modules:
  0.0 289.1 jit_solution(16227011751404007670)
XLA Ops:
  0.7 0.8 compare_select_fusion.1
  1.4 0.7 compare_select_fusion
  2.1 4.0 %gather_fusion = bf16[64,2,36,128]{3,1,2,0:T(2,128)(2,1)S(1)} fusion(bf16[2,36,64,128]{3,0,2,1:T(2,128)(2,1)S(1)} %bitcast.22, s32[1024]{0:T(1024)S(1)} %get-tuple-element.35), kind=kCustom, calls=%fused_computation | custom fusion | bytes 2359552 | tf_op jit(solution)/shard_map/gather | solution.py:86
  6.2 0.3 copy.68
  6.5 0.4 reshape_reshape.12
  7.0 1.1 copy.69
  8.1 7.5 %all-to-all-start = ((bf16[32,2,16,1,1,256]{5,2,1,4,3,0:T(8,128)(2,1)}), bf16[32,2,16,1,1,256]{5,2,1,4,3,0:T(8,128)(2,1)S(1)}, u32[]{:S(2)}, u32[]{:S(2)}) async-start(bf16[32,2,16,1,1,256]{5,2,1,4,3,0:T(8,128)(2,1)} %copy.69), calls=%async_computation | async-start | bytes 1048576 | tf_op jit(solution)/shard_map/all_to_all | solution.py:41
  15.7 1.5 copy.70
  17.2 8.5 %all-to-all-done = bf16[32,2,16,1,1,256]{5,2,1,4,3,0:T(8,128)(2,1)S(1)} async-done(((bf16[32,2,16,1,1,256]{5,2,1,4,3,0:T(8,128)(2,1)}), bf16[32,2,16,1,1,256]{5,2,1,4,3,0:T(8,128)(2,1)S(1)}, u32[]{:S(2)}, u32[]{:S(2)}) %all-to-all-start) | async-done | bytes 524320 | tf_op jit(solution)/shard_map/all_to_all | solution.py:41
  25.6 5.2 %all-to-all-start.1 = ((bf16[32,2,20,1,1,256]{5,1,4,3,2,0:T(2,128)(2,1)}), bf16[32,2,20,1,1,256]{5,1,4,3,2,0:T(2,128)(2,1)S(1)}, u32[]{:S(2)}, u32[]{:S(2)}) async-start(bf16[32,2,20,1,1,256]{5,1,4,3,2,0:T(2,128)(2,1)} %copy.70), calls=%async_computation.1 | async-start | bytes 1310720 | tf_op jit(solution)/shard_map/all_to_all | solution.py:41
  30.8 24.3 %reshape_reshape.14 = bf16[2,36,2,32,1,1152]{5,3,2,0,1,4:T(8,128)(2,1)} reshape(bf16[2,36,73728]{2,0,1:T(2,128)(2,1)} %param.7) | data formatting | bytes 21233664 | tf_op jit(solution)/shard_map/reshape;reshape | solution.py:18
  55.2 5.1 %split.18 = bf16[32,2,16,2,1,1152]{5,0,3,1,2,4:T(8,128)(2,1)} slice(bf16[32,2,36,2,1,1152]{5,0,3,1,2,4:T(8,128)(2,1)} %bitcast.23), slice={[0:32], [0:2], [0:16], [0:2], [0:1], [0:1152]} | slice | bytes 9437184 | tf_op jit(solution)/shard_map/split | solution.py:39
  60.2 9.5 %copy.72 = bf16[32,2,16,2,1,1152]{5,3,2,1,4,0:T(2,128)(2,1)} copy(bf16[32,2,16,2,1,1152]{5,0,3,1,2,4:T(8,128)(2,1)} %split.18) | data formatting | bytes 9437184 | tf_op jit(solution)/shard_map/split | solution.py:39
  69.7 7.4 %all-to-all-start.2 = ((bf16[32,2,16,2,1,1152]{5,3,2,1,4,0:T(2,128)(2,1)}), bf16[32,2,16,2,1,1152]{5,3,2,1,4,0:T(2,128)(2,1)}, u32[]{:S(2)}, u32[]{:S(2)}) async-start(bf16[32,2,16,2,1,1152]{5,3,2,1,4,0:T(2,128)(2,1)} %copy.72), calls=%async_computation.2 | async-start | bytes 9437184 | tf_op jit(solution)/shard_map/all_to_all | solution.py:41
  77.1 3.4 %split.19 = bf16[32,2,20,2,1,1152]{5,0,3,1,2,4:T(8,128)(2,1)S(1)} slice(bf16[32,2,36,2,1,1152]{5,0,3,1,2,4:T(8,128)(2,1)} %bitcast.24), slice={[0:32], [0:2], [16:36], [0:2], [0:1], [0:1152]} | slice | bytes 11796480 | tf_op jit(solution)/shard_map/split | solution.py:39
  80.5 7.4 %copy.73 = bf16[32,2,20,2,1,1152]{5,3,2,1,4,0:T(2,128)(2,1)} copy(bf16[32,2,20,2,1,1152]{5,0,3,1,2,4:T(8,128)(2,1)S(1)} %split.19) | data formatting | bytes 11796480 | tf_op jit(solution)/shard_map/split | solution.py:39
  87.9 51.0 %all-to-all-done.2 = bf16[32,2,16,2,1,1152]{5,3,2,1,4,0:T(2,128)(2,1)} async-done(((bf16[32,2,16,2,1,1152]{5,3,2,1,4,0:T(2,128)(2,1)}), bf16[32,2,16,2,1,1152]{5,3,2,1,4,0:T(2,128)(2,1)}, u32[]{:S(2)}, u32[]{:S(2)}) %all-to-all-start.2) | async-done | bytes 4718624 | tf_op jit(solution)/shard_map/all_to_all | solution.py:41
  138.9 4.7 %all-to-all-start.3 = ((bf16[32,2,20,2,1,1152]{5,3,2,1,4,0:T(2,128)(2,1)}), bf16[32,2,20,2,1,1152]{5,3,2,1,4,0:T(2,128)(2,1)}, u32[]{:S(2)}, u32[]{:S(2)}) async-start(bf16[32,2,20,2,1,1152]{5,3,2,1,4,0:T(2,128)(2,1)} %copy.73), calls=%async_computation.3 | async-start | bytes 11796480 | tf_op jit(solution)/shard_map/all_to_all | solution.py:41
  144.1 0.2 fusion.2
  144.3 0.4 copy_dynamic-update-slice_fusion
  144.7 0.5 constant_dynamic-update-slice_fusion
  145.2 1.2 convert_reduce_fusion.1
  146.7 77.8 %all-to-all-done.3 = bf16[32,2,20,2,1,1152]{5,3,2,1,4,0:T(2,128)(2,1)} async-done(((bf16[32,2,20,2,1,1152]{5,3,2,1,4,0:T(2,128)(2,1)}), bf16[32,2,20,2,1,1152]{5,3,2,1,4,0:T(2,128)(2,1)}, u32[]{:S(2)}, u32[]{:S(2)}) %all-to-all-start.3) | async-done | bytes 5898272 | tf_op jit(solution)/shard_map/all_to_all | solution.py:41
  224.5 21.4 %convert_reduce_fusion = (f32[2,2,1152]{2,1,0:T(2,128)S(1)}, bf16[2,32,36,2,1,1152]{5,3,2,0,4,1:T(2,128)(2,1)}) fusion(bf16[32,2,20,2,1,1152]{5,3,2,1,4,0:T(2,128)(2,1)} %all-to-all-done.3, bf16[32,2,16,2,1,1152]{5,3,2,1,4,0:T(2,128)(2,1)} %all-to-all-done.2), kind=kLoop, calls=%fused_computation.2 | loop fusion | flops 15920640 | bytes 21252096 | tf_op jit(solution)/shard_map/reduce_sum | solution.py:72
  246.2 0.5 broadcast_in_dim.12
  246.7 5.4 %all-to-all-start.4 = ((f32[4,1,40]{2,1,0:T(1,128)}), f32[4,1,40]{2,1,0:T(1,128)S(1)}, u32[]{:S(2)}, u32[]{:S(2)}) async-start(f32[4,1,40]{2,1,0:T(1,128)} %broadcast_in_dim.12), calls=%async_computation.4 | async-start | bytes 4096 | tf_op jit(solution)/shard_map/all_to_all | solution.py:47
  252.3 0.6 gather_fusion.1
  252.8 1.2 copy.79
  254.0 10.2 %copy.74 = bf16[2,32,36,2,1,1152]{5,3,2,1,0,4:T(2,128)(2,1)} copy(bf16[2,32,36,2,1,1152]{5,3,2,0,4,1:T(2,128)(2,1)} %get-tuple-element.33) | data formatting | bytes 21233664 | tf_op jit(solution)/shard_map/transpose | solution.py:32
  264.2 23.2 %reshape_reshape.15 = bf16[2,1152,2304]{2,1,0:T(8,128)(2,1)} reshape(bf16[2,32,36,2,1,1152]{5,3,2,1,0,4:T(2,128)(2,1)} %copy.74) | data formatting | bytes 21233664 | tf_op jit(solution)/shard_map/reshape;reshape | solution.py:68
  287.8 0.7 copy.80
  288.4 0.6 multiply_subtract_fusion
  (32 shorter events, 1.5 us)
Async XLA Ops:
  0.6 1.5 copy-start
  8.1 17.6 %all-to-all-start = ((bf16[32,2,16,1,1,256]{5,2,1,4,3,0:T(8,128)(2,1)}), bf16[32,2,16,1,1,256]{5,2,1,4,3,0:T(8,128)(2,1)S(1)}, u32[]{:S(2)}, u32[]{:S(2)}) async-start(bf16[32,2,16,1,1,256]{5,2,1,4,3,0:T(8,128)(2,1)} %copy.69), calls=%async_computation | async-start | bytes 1048576 | tf_op jit(solution)/shard_map/all_to_all | solution.py:41
  25.6 44.1 %all-to-all-start.1 = ((bf16[32,2,20,1,1,256]{5,1,4,3,2,0:T(2,128)(2,1)}), bf16[32,2,20,1,1,256]{5,1,4,3,2,0:T(2,128)(2,1)S(1)}, u32[]{:S(2)}, u32[]{:S(2)}) async-start(bf16[32,2,20,1,1,256]{5,1,4,3,2,0:T(2,128)(2,1)} %copy.70), calls=%async_computation.1 | async-start | bytes 1310720 | tf_op jit(solution)/shard_map/all_to_all | solution.py:41
  69.7 69.2 %all-to-all-start.2 = ((bf16[32,2,16,2,1,1152]{5,3,2,1,4,0:T(2,128)(2,1)}), bf16[32,2,16,2,1,1152]{5,3,2,1,4,0:T(2,128)(2,1)}, u32[]{:S(2)}, u32[]{:S(2)}) async-start(bf16[32,2,16,2,1,1152]{5,3,2,1,4,0:T(2,128)(2,1)} %copy.72), calls=%async_computation.2 | async-start | bytes 9437184 | tf_op jit(solution)/shard_map/all_to_all | solution.py:41
  87.9 55.7 %copy-start.2 = (s32[46,576]{1,0:T(8,128)S(1)}, s32[46,576]{1,0:T(8,128)}, u32[]{:S(2)}) copy-start(s32[46,576]{1,0:T(8,128)} %param.11) | copy-start | bytes 317956
  87.9 55.7 %copy-start.3 = (s32[2]{0:T(128)S(1)}, s32[2]{0:T(128)}, u32[]{:S(2)}) copy-start(s32[2]{0:T(128)} %param.9) | copy-start | bytes 28
  87.9 56.2 %copy-start.4 = (s32[46,64]{1,0:T(8,128)S(1)}, s32[46,64]{1,0:T(8,128)}, u32[]{:S(2)}) copy-start(s32[46,64]{1,0:T(8,128)} %param.10) | copy-start | bytes 35332
  138.9 85.5 %all-to-all-start.3 = ((bf16[32,2,20,2,1,1152]{5,3,2,1,4,0:T(2,128)(2,1)}), bf16[32,2,20,2,1,1152]{5,3,2,1,4,0:T(2,128)(2,1)}, u32[]{:S(2)}, u32[]{:S(2)}) async-start(bf16[32,2,20,2,1,1152]{5,3,2,1,4,0:T(2,128)(2,1)} %copy.73), calls=%async_computation.3 | async-start | bytes 11796480 | tf_op jit(solution)/shard_map/all_to_all | solution.py:41
  246.7 40.7 %all-to-all-start.4 = ((f32[4,1,40]{2,1,0:T(1,128)}), f32[4,1,40]{2,1,0:T(1,128)S(1)}, u32[]{:S(2)}, u32[]{:S(2)}) async-start(f32[4,1,40]{2,1,0:T(1,128)} %broadcast_in_dim.12), calls=%async_computation.4 | async-start | bytes 4096 | tf_op jit(solution)/shard_map/all_to_all | solution.py:47
  264.2 24.8 %copy-start.1 = (bf16[2,36,8192]{2,0,1:T(2,128)(2,1)S(1)}, bf16[2,36,8192]{2,0,1:T(2,128)(2,1)}, u32[]{:S(2)}) copy-start(bf16[2,36,8192]{2,0,1:T(2,128)(2,1)} %param.6) | copy-start | bytes 3538948
where the time goes:
time: 291 us; the launch traced here: 289 us
  waiting for transfers between devices  137 us (47%)
  local copies, waits for them, and re-layouts  95.2 us (33%)
  starting transfers between devices  30.3 us (10%)
  other arithmetic  25.1 us (9%)
    all_to_all x4, waiting for transfers between devices, several_exchanges(): lax.all_to_all(piece, axis, split_axis=0, concat_axis=0, tiled=True)  137 us
    split x8, local copies, waits for them, and re-layouts, several_exchanges(): jnp.split(blocks, piece_ends(blocks.shape[split_at], pieces), axis=split_at)  28 us
    all_to_all x4, starting transfers between devices, several_exchanges(): lax.all_to_all(piece, axis, split_axis=0, concat_axis=0, tiled=True)  24.8 us
    another operation x2, local copies, waits for them, and re-layouts, cut_along(): x.reshape(*dims[:dim], length, dims[dim] // length, *dims[dim + 1:])  24.8 us
    another operation x1, local copies, waits for them, and re-layouts, finish(): served_gate = gate_piece.reshape(count, height, 2 * gate_piece.shape[4])  23.2 us
    reduce_sum x2, other arithmetic, finish(): jnp.sum(served_gate.astype(jnp.float32).reshape(count, height, -1, BLK),...  21.5 us
    transpose x1, local copies, waits for them, and re-layouts, in_order(): return jnp.moveaxis(blocks, 0, dim).reshape(dims)  10.2 us
  transfers between devices with their start and end apart: 5, of which 3 were waited for; matrix products, arithmetic and copies ran while one was open for 31% of the time, Pallas kernels for 0%

commit v1 on v0

v1 whole, which is shorter than its diff:
```python
import functools

import jax
import jax.numpy as jnp
import numpy as np
from jax import lax
from jax.experimental import pallas as pl
from jax.experimental.pallas import tpu as pltpu
from jax.sharding import PartitionSpec as P


HEAD_DIM = 128
FF = 36864
STORED = 46
BLK = 128
NHEAD = 64

stored_unit = 1.0 / 1024.0

ORDER = [(1, 0), (3, 0), (0, 1), (0, 3), (1, 1), (3, 3), (1, 3), (3, 1), (2, 0), (0, 2), (2, 1), (2, 3), (1, 2), (3, 2), (2, 2)]

MOVES = [(dx, dy, dc) for dx, dy in ORDER for dc in (0, 1)] + [(0, 0, 1), (0, 0, 0)]
COUNTS = [2, 4, 6, 8, 12]

ROWS = 36
TILES = FF // 32 // 128
PIECE = (2 * ROWS + 8, TILES, 2, 128)
GATE_ROWS = ROWS * TILES * 2
HEAD_ROWS = ROWS * 2


def place_of(me):
    return me // 8, (me // 2) % 4, me % 2


def moved_pairs(dx, dy, dc):
    pairs = []
    for me in range(32):
        x, y, c = place_of(me)
        pairs.append((me, (((x + dx) % 4) * 4 + (y + dy) % 4) * 2 + (c ^ dc)))
    return pairs


def in_hbm(x):
    return pltpu.with_memory_space_constraint(x, pltpu.HBM)


def in_vmem(x):
    return pltpu.with_memory_space_constraint(x, pltpu.VMEM)


def here():
    me = lax.axis_index("dev")
    return lax.div(me, 8), lax.rem(lax.div(me, 2), 4), lax.rem(me, 2)


def cut_kernel(shifts, heads, gate, qkv, *rest):
    outs, (held, in_sems, out_sems) = rest[-3 - len(shifts) : -3], rest[-3:]
    x, y, c = here()
    loads = []
    for i, (dx, dy, dc) in enumerate(shifts):
        owner = (lax.rem(x + dx, 4) * 4 + lax.rem(y + dy, 4)) * 2 + lax.rem(c + dc, 2)
        loads.append(
            [
                pltpu.make_async_copy(
                    gate.at[:, pl.ds(p * 32 * TILES + owner * TILES, TILES)],
                    held.at[i, pl.ds(p * ROWS, ROWS)],
                    in_sems.at[i, p],
                )
                for p in range(2)
            ]
            + [
                pltpu.make_async_copy(
                    qkv.at[:, :, heads[2 * owner + k]],
                    held.at[i, pl.ds(2 * ROWS + 4 * k, 4)],
                    in_sems.at[i, 2 + k],
                )
                for k in range(2)
            ]
        )
    stores = [pltpu.make_async_copy(held.at[i], out, out_sems.at[i]) for i, out in enumerate(outs)]
    for load in loads:
        for copy in load:
            copy.start()
    for load, store in zip(loads, stores):
        for copy in load:
            copy.wait()
        store.start()
    for store in stores:
        store.wait()


def cut(shifts, heads, gate, qkv, after):
    size = int(np.prod(PIECE)) * 2 * len(shifts)
    return pl.pallas_call(
        functools.partial(cut_kernel, shifts),
        out_shape=[pltpu.HBM(PIECE, jnp.bfloat16)] * len(shifts),
        in_specs=[pl.BlockSpec(memory_space=pltpu.SMEM)] + [pl.BlockSpec(memory_space=pl.ANY)] * (2 + len(after)),
        out_specs=[pl.BlockSpec(memory_space=pl.ANY)] * len(shifts),
        scratch_shapes=[
            pltpu.VMEM((len(shifts), *PIECE), jnp.bfloat16),
            pltpu.SemaphoreType.DMA((len(shifts), 4)),
            pltpu.SemaphoreType.DMA((len(shifts),)),
        ],
        compiler_params=pltpu.CompilerParams(vmem_limit_bytes=(len(shifts) + 1) << 19),
        cost_estimate=pl.CostEstimate(flops=size, bytes_accessed=2 * size, transcendentals=0),
        name="cut",
    )(heads, gate, qkv, *after)


def turns():
    gate = np.zeros((168, 144), np.float32)
    for r in range(8):
        for j in range(TILES):
            for l in range(2):
                k = (r * TILES + j) * 2 + l
                gate[l * 72 + j * 8 + r, k] = 1
                gate[144 + l * TILES + j, k] = 1
    head = np.zeros((2, 152, 72), np.float32)
    for r in range(72):
        for l in range(2):
            part, k = r // 36, (r % 36) * 2 + l
            head[part, l * 72 + r, k] = 1
            head[part, 144 + l, k] = 1
    return jnp.asarray(gate, jnp.bfloat16), jnp.asarray(head, jnp.bfloat16)


def serve_kernel(shift, turn, head_turn, same, other, gate_in, qkv_in, sums_in, gate_out, qkv_out, sums, held, held_heads, gate_buf, qkv_buf, in_sems, out_sems):
    del gate_in, qkv_in
    x, y, c = here()
    chip = lax.rem(x + 4 - shift[0], 4) * 4 + lax.rem(y + 4 - shift[1], 4)
    copies = []
    for i, piece in enumerate((same, other)):
        slot = c if i == 0 else 1 - c
        for p in range(2):
            copies.append(
                pltpu.make_async_copy(
                    piece.at[pl.ds(p * GATE_ROWS, GATE_ROWS)],
                    held.at[slot, p, pl.ds(pl.multiple_of(slot * 8, 8), GATE_ROWS)],
                    in_sems.at[i, p],
                )
            )
        copies.append(
            pltpu.make_async_copy(
                piece.at[pl.ds(2 * GATE_ROWS, 2 * HEAD_ROWS)], held_heads.at[slot], in_sems.at[i, 2]
            )
        )
    for copy in copies:
        copy.start()
    for copy in copies:
        copy.wait()

    def both(slot, start, length):
        return jnp.concatenate([held[slot, p, pl.ds(start, length)] for p in range(2)], axis=1)

    def dot(a, b):
        return jnp.dot(a, b, preferred_element_type=jnp.float32)

    gate_sum = jnp.zeros((24, 256), jnp.float32)
    for g in range(9):
        if g < 4:
            got = dot(turn[...], both(0, 144 * g, 144))
        elif g > 4:
            got = dot(turn[...], both(1, 80 + 144 * (g - 5), 144))
        else:
            got = dot(turn[:, :72], both(0, 576, 72)) + dot(turn[:, 72:], both(1, 8, 72))
        for l in range(2):
            for p in range(2):
                gate_buf[l, pl.ds(144 * g + 72 * p, 72), :] = got[l * 72 : (l + 1) * 72, p * 128 : (p + 1) * 128].astype(jnp.bfloat16)
        gate_sum += got[144:168]
    got = None
    for part in range(2):
        heads = jnp.concatenate([held_heads[part, pl.ds(72 * k, 72)] for k in range(2)], axis=1)
        term = dot(head_turn[part], heads)
        got = term if got is None else got + term
    for l in range(2):
        for g in range(9):
            for k in range(2):
                qkv_buf[l, pl.ds(16 * g + 8 * k, 8), :] = got[l * 72 + 8 * g : l * 72 + 8 * g + 8, k * 128 : (k + 1) * 128].astype(jnp.bfloat16)
    head_sum = got[144:152]
    if sums_in is not None:
        gate_sum = gate_sum + sums_in[0:24, :]
        head_sum = head_sum + sums_in[24:32, :]
    sums[0:24, :] = gate_sum
    sums[24:32, :] = head_sum
    out = [
        pltpu.make_async_copy(gate_buf, gate_out.at[:, pl.ds(pl.multiple_of(chip * 1296, 16), 1296)], out_sems.at[0]),
        pltpu.make_async_copy(qkv_buf, qkv_out.at[:, pl.ds(pl.multiple_of(chip * 144, 16), 144)], out_sems.at[1]),
    ]
    for copy in out:
        copy.start()
    for copy in out:
        copy.wait()


def serve(shift, turn, head_turn, same, other, done):
    first = done is None
    any_spec = pl.BlockSpec(memory_space=pl.ANY)
    vmem_spec = pl.BlockSpec(memory_space=pltpu.VMEM)
    kernel = functools.partial(serve_kernel, shift)
    if first:
        kernel = lambda a, b, c, d, *rest: serve_kernel(shift, a, b, c, d, None, None, None, *rest)
    pieces = [same.reshape(1440, 128), other.reshape(1440, 128)]
    pieces = [in_hbm(piece) for piece in pieces]
    return pl.pallas_call(
        kernel,
        out_shape=[
            pltpu.HBM((2, 16 * 1296, 128), jnp.bfloat16),
            pltpu.HBM((2, 16 * 144, 128), jnp.bfloat16),
            pltpu.VMEM((32, 256), jnp.float32),
        ],
        in_specs=[vmem_spec, vmem_spec, any_spec, any_spec] + ([] if first else [any_spec, any_spec, vmem_spec]),
        out_specs=[any_spec, any_spec, vmem_spec],
        scratch_shapes=[
            pltpu.VMEM((2, 2, 656, 128), jnp.bfloat16),
            pltpu.VMEM((2, 144, 128), jnp.bfloat16),
            pltpu.VMEM((2, 1296, 128), jnp.bfloat16),
            pltpu.VMEM((2, 144, 128), jnp.bfloat16),
            pltpu.SemaphoreType.DMA((2, 3)),
            pltpu.SemaphoreType.DMA((2,)),
        ],
        input_output_aliases={} if first else {4: 0, 5: 1},
        compiler_params=pltpu.CompilerParams(vmem_limit_bytes=8 << 20),
        cost_estimate=pl.CostEstimate(flops=2 * 168 * 144 * 256 * 10, bytes_accessed=3 << 20, transcendentals=0),
        name="serve",
    )(turn, head_turn, *pieces, *(() if first else done))


def relayout(qkv_weight, gate_up_weight, head_slot, layer_ids, stored_qkv, stored_gate_up):
    owners = lax.axis_size("dev")
    owner = lax.axis_index("dev")
    layers = qkv_weight.shape[0]
    slots = NHEAD // owners
    blocks = FF // owners // BLK
    gate = gate_up_weight.transpose(1, 0, 2).reshape(ROWS, 2, 2 * FF // 128, 128).transpose(0, 2, 1, 3)
    qkv = qkv_weight.transpose(1, 0, 2).reshape(4, 9, 2, NHEAD, HEAD_DIM).transpose(0, 1, 3, 2, 4)

    moves = MOVES
    gate, qkv = in_hbm(gate), in_vmem(qkv)
    pieces = {}
    at, after = 0, ()
    for count in COUNTS:
        part = tuple(moves[at : at + count])
        made = cut(part, head_slot, gate, qkv, after)
        pieces.update(zip(part, made))
        at, after = at + count, (made[-1],)
    got = {}
    for move in moves[:-1]:
        got[move] = lax.ppermute(pieces[move], "dev", moved_pairs(*move))
    got[(0, 0, 0)] = pieces[(0, 0, 0)]

    turn, head_turn = turns()
    done = None
    for shift in [(0, 0)] + ORDER:
        done = serve(shift, turn, head_turn, got[(*shift, 0)], got[(*shift, 1)], done)
    gate_out, qkv_out, total = done
    served_qkv = qkv_out.reshape(2, 144, 2, 8, 128).transpose(0, 1, 3, 2, 4).reshape(2, 1152, 256)
    served_gate = gate_out.reshape(2, 144, 18, 8, 128).transpose(0, 1, 3, 2, 4).reshape(2, 1152, 2304)

    lane = jnp.sum(total.reshape(32, 2, 128), axis=2)
    for step in (2, 1):
        lane = lane + lax.ppermute(lane, "grp", [(g, g ^ step) for g in range(4)])
    block_sum = lane[:18].reshape(2, 9, 2).transpose(0, 2, 1).reshape(2, 18)
    head_sum = lane[24:26]

    layer_pick = (layer_ids[:, None] == jnp.arange(STORED, dtype=jnp.int32)[None, :]).astype(jnp.float32)
    picked_qkv = jnp.dot(layer_pick, stored_qkv.astype(jnp.float32), precision=lax.Precision.HIGHEST, preferred_element_type=jnp.float32)
    picked_gate = jnp.dot(layer_pick, stored_gate_up.astype(jnp.float32), precision=lax.Precision.HIGHEST, preferred_element_type=jnp.float32)
    own_heads = lax.dynamic_slice_in_dim(head_slot, owner * slots, slots, 0)
    picked_qkv = picked_qkv[:, own_heads]
    picked_gate = picked_gate.reshape(layers, 2, owners, blocks).transpose(0, 2, 1, 3).reshape(layers, owners * 2 * blocks)
    picked_gate = lax.dynamic_slice_in_dim(picked_gate, owner * 2 * blocks, 2 * blocks, 1)
    qkv_mismatch = head_sum - picked_qkv * stored_unit
    gate_up_mismatch = block_sum - picked_gate * stored_unit
    return served_qkv, served_gate, qkv_mismatch, gate_up_mismatch


def solution(mesh):
    placed = (P(None, ("grp", "dev"), None), P(None, ("grp", "dev"), None), P(), P(), P(), P())
    return jax.shard_map(
        relayout,
        mesh=mesh,
        in_specs=placed,
        out_specs=(P(None, "grp", "dev"), P(None, "grp", "dev"), P(None, "dev"), P(None, "dev")),
        check_vma=False,
    )
```

time: 291 us -> 238 us (0.82)
  the two profiles are of different devices: /device:TPU:40 before, /device:TPU:4 now
where the time goes in v1:
time: 238 us; the launch traced here: 237 us
  starting transfers between devices  114 us (48%)
  Pallas kernels  59 us (25%)
  waiting for transfers between devices  49.5 us (21%)
  local copies, waits for them, and re-layouts  10.2 us (4%)
    ppermute x31, starting transfers between devices, relayout(): got[move] = lax.ppermute(pieces[move], 'dev', moved_pairs(*move))  109 us
    ppermute x31, waiting for transfers between devices, relayout(): got[move] = lax.ppermute(pieces[move], 'dev', moved_pairs(*move))  46.7 us
    pallas_call x16, Pallas kernels, serve(): pl.pallas_call(kernel, out_shape=[pltpu.HBM((2, 16 * 1296, 128), jnp.bflo...  41.3 us
    pallas_call x5, Pallas kernels, cut(): pl.pallas_call(functools.partial(cut_kernel, shifts), out_shape=[pltpu.HB...  17.7 us
    unnamed x89, local copies, waits for them, and re-layouts  9.07 us
    ppermute x2, starting transfers between devices, relayout(): lane = lane + lax.ppermute(lane, 'grp', [(g, g ^ step) for g in range(4)])  5.57 us
  transfers between devices with their start and end apart: 33, of which 13 were waited for; matrix products, arithmetic and copies ran while one was open for 1% of the time, Pallas kernels for 16%

profile of v1, /device:TPU:4, one launch (start us, length us, event | category | flops | bytes accessed | tf_op | source)
XLA Modules:
  0.0 237.2 jit_solution(17971003550763091407)
XLA Ops:
  6.2 2.9 %cut.6 = (bf16[80,9,2,128]{3,2,1,0:T(2,128)(2,1)}, bf16[80,9,2,128]{3,2,1,0:T(2,128)(2,1)}, bf16[80,9,2,128]{3,2,1,0:T(2,128)(2,1)}, bf16[80,9,2,128]{3,2,1,0:T(2,128)(2,1)}) custom-call(s32[64]{0:T(128)S(1)} %copy-done.12, bf16[36,576,2,128]{3,2,1,0:T(2,128)(2,1)} %bitcast.67, bf16[4,9,64,2,128]{4,3,2,1,0:T(2,128)(2,1)S(1)} %bitcast.60, ...), custom_call_target="tpu_custom_call" | custom-call | flops 1474560 | bytes 2949120 | tf_op jit(solution)/shard_map/cut/pallas_call | solution.py:95
  10.1 3.3 %cut.7 = (bf16[80,9,2,128]{3,2,1,0:T(2,128)(2,1)}, bf16[80,9,2,128]{3,2,1,0:T(2,128)(2,1)}, bf16[80,9,2,128]{3,2,1,0:T(2,128)(2,1)}, bf16[80,9,2,128]{3,2,1,0:T(...) custom-call(s32[64]{0:T(128)S(1)} %copy-done.12, bf16[36,576,2,128]{3,2,1,0:T(2,128)(2,1)} %bitcast.68, ...), custom_call_target="tpu_custom_call" | custom-call | flops 2211840 | bytes 4423680 | tf_op jit(solution)/shard_map/cut/pallas_call | solution.py:95
  14.4 3.7 %cut.8 = (bf16[80,9,2,128]{3,2,1,0:T(2,128)(2,1)}, bf16[80,9,2,128]{3,2,1,0:T(2,128)(2,1)}, bf16[80,9,2,128]{3,2,1,0:T(2,128)(2,1)}, bf16[80,9,2,128]{3,2,1,0:T(...) custom-call(s32[64]{0:T(128)S(1)} %copy-done.12, ...), custom_call_target="tpu_custom_call" | custom-call | flops 2949120 | bytes 5898240 | tf_op jit(solution)/shard_map/cut/pallas_call | solution.py:95
  19.2 5.2 %cut.9 = (bf16[80,9,2,128]{3,2,1,0:T(2,128)(2,1)}, bf16[80,9,2,128]{3,2,1,0:T(2,128)(2,1)}, bf16[80,9,2,128]{3,2,1,0:T(2,128)(2,1)}, bf16[80,9,2,128]{3,2,1,0:T(...) custom-call(s32[64]{0:T(128)S(1)} %copy-done.12, ...), custom_call_target="tpu_custom_call" | custom-call | flops 4423680 | bytes 8847360 | tf_op jit(solution)/shard_map/cut/pallas_call | solution.py:95
  24.4 3.9 %collective-permute-start.4 = (bf16[80,9,2,128]{3,2,1,0:T(2,128)(2,1)}, bf16[80,9,2,128]{3,2,1,0:T(2,128)(2,1)S(1)}, u32[]{:S(2)}, u32[]{:S(2)}) collective-permute-start(bf16[80,9,2,128]{3,2,1,0:T(2,128)(2,1)} %get-tuple-element.92), channel_id=1, source_target_pairs={{0,12},{1,13},{2,14},{3,15},{4,8},{5,9},{6,10},{7,11},{8,20},{9,21... | collective-permute-start | bytes 1105928 | tf_op jit(solution)/shard_map/ppermute | solution.py:249
  32.9 3.7 %collective-permute-start.9 = (bf16[80,9,2,128]{3,2,1,0:T(2,128)(2,1)}, bf16[80,9,2,128]{3,2,1,0:T(2,128)(2,1)S(1)}, u32[]{:S(2)}, u32[]{:S(2)}) collective-permute-start(bf16[80,9,2,128]{3,2,1,0:T(2,128)(2,1)} %get-tuple-element.97), channel_id=1, source_target_pairs={{0,19},{1,18},{2,21},{3,20},{4,23},{5,22},{6,17},{7,16},{8,27},{9,... | collective-permute-start | bytes 1105928 | tf_op jit(solution)/shard_map/ppermute | solution.py:249
  38.6 3.2 %collective-permute-start.10 = (bf16[80,9,2,128]{3,2,1,0:T(2,128)(2,1)S(1)}, bf16[80,9,2,128]{3,2,1,0:T(2,128)(2,1)S(1)}, u32[]{:S(2)}, u32[]{:S(2)}) collective-permute-start(bf16[80,9,2,128]{3,2,1,0:T(2,128)(2,1)S(1)} %copy-done.43), channel_id=1, source_target_pairs={{0,4},{1,5},{2,6},{3,7},{4,0},{5,1},{6,2},{7,3},{8,12},{9,13},{10,... | collective-permute-start | bytes 1105928 | tf_op jit(solution)/shard_map/ppermute | solution.py:249
  41.8 8.0 %collective-permute-done.6 = bf16[80,9,2,128]{3,2,1,0:T(2,128)(2,1)S(1)} collective-permute-done((bf16[80,9,2,128]{3,2,1,0:T(2,128)(2,1)}, bf16[80,9,2,128]{3,2,1,0:T(2,128)(2,1)S(1)}, u32[]{:S(2)}, u32[]{:S(2)}) %collective-permute-start.6) | collective-permute-done | bytes 368672 | tf_op jit(solution)/shard_map/ppermute | solution.py:249
  50.8 4.9 %collective-permute-done.7 = bf16[80,9,2,128]{3,2,1,0:T(2,128)(2,1)S(1)} collective-permute-done((bf16[80,9,2,128]{3,2,1,0:T(2,128)(2,1)}, bf16[80,9,2,128]{3,2,1,0:T(2,128)(2,1)S(1)}, u32[]{:S(2)}, u32[]{:S(2)}) %collective-permute-start.7) | collective-permute-done | bytes 368672 | tf_op jit(solution)/shard_map/ppermute | solution.py:249
  55.7 5.2 %collective-permute-start.12 = (bf16[80,9,2,128]{3,2,1,0:T(2,128)(2,1)S(1)}, bf16[80,9,2,128]{3,2,1,0:T(2,128)(2,1)S(1)}, u32[]{:S(2)}, u32[]{:S(2)}) collective-permute-start(bf16[80,9,2,128]{3,2,1,0:T(2,128)(2,1)S(1)} %copy-done.42), channel_id=1, source_target_pairs={{0,16},{1,17},{2,18},{3,19},{4,20},{5,21},{6,22},{7,23},{8,24},{9,... | collective-permute-start | bytes 1105928 | tf_op jit(solution)/shard_map/ppermute | solution.py:249
  60.9 6.8 %collective-permute-done.8 = bf16[80,9,2,128]{3,2,1,0:T(2,128)(2,1)S(1)} collective-permute-done((bf16[80,9,2,128]{3,2,1,0:T(2,128)(2,1)}, bf16[80,9,2,128]{3,2,1,0:T(2,128)(2,1)S(1)}, u32[]{:S(2)}, u32[]{:S(2)}) %collective-permute-start.8) | collective-permute-done | bytes 368672 | tf_op jit(solution)/shard_map/ppermute | solution.py:249
  67.7 3.5 %collective-permute-start.13 = (bf16[80,9,2,128]{3,2,1,0:T(2,128)(2,1)S(1)}, bf16[80,9,2,128]{3,2,1,0:T(2,128)(2,1)S(1)}, u32[]{:S(2)}, u32[]{:S(2)}) collective-permute-start(bf16[80,9,2,128]{3,2,1,0:T(2,128)(2,1)S(1)} %copy-done.41), channel_id=1, source_target_pairs={{0,17},{1,16},{2,19},{3,18},{4,21},{5,20},{6,23},{7,22},{8,25},{9,... | collective-permute-start | bytes 1105928 | tf_op jit(solution)/shard_map/ppermute | solution.py:249
  71.2 4.7 %collective-permute-done.9 = bf16[80,9,2,128]{3,2,1,0:T(2,128)(2,1)S(1)} collective-permute-done((bf16[80,9,2,128]{3,2,1,0:T(2,128)(2,1)}, bf16[80,9,2,128]{3,2,1,0:T(2,128)(2,1)S(1)}, u32[]{:S(2)}, u32[]{:S(2)}) %collective-permute-start.9) | collective-permute-done | bytes 368672 | tf_op jit(solution)/shard_map/ppermute | solution.py:249
  76.0 5.0 %collective-permute-start.15 = (bf16[80,9,2,128]{3,2,1,0:T(2,128)(2,1)S(1)}, bf16[80,9,2,128]{3,2,1,0:T(2,128)(2,1)S(1)}, u32[]{:S(2)}, u32[]{:S(2)}) collective-permute-start(bf16[80,9,2,128]{3,2,1,0:T(2,128)(2,1)S(1)} %copy-done.39), channel_id=1, source_target_pairs={{0,27},{1,26},{2,29},{3,28},{4,31},{5,30},{6,25},{7,24},{8,3},{9,2... | collective-permute-start | bytes 1105928 | tf_op jit(solution)/shard_map/ppermute | solution.py:249
  82.1 5.2 %collective-permute-start.17 = (bf16[80,9,2,128]{3,2,1,0:T(2,128)(2,1)S(1)}, bf16[80,9,2,128]{3,2,1,0:T(2,128)(2,1)S(1)}, u32[]{:S(2)}, u32[]{:S(2)}) collective-permute-start(bf16[80,9,2,128]{3,2,1,0:T(2,128)(2,1)S(1)} %copy-done.37), channel_id=1, source_target_pairs={{0,15},{1,14},{2,9},{3,8},{4,11},{5,10},{6,13},{7,12},{8,23},{9,22... | collective-permute-start | bytes 1105928 | tf_op jit(solution)/shard_map/ppermute | solution.py:249
  89.3 6.0 %collective-permute-done.14 = bf16[80,9,2,128]{3,2,1,0:T(2,128)(2,1)S(1)} collective-permute-done((bf16[80,9,2,128]{3,2,1,0:T(2,128)(2,1)S(1)}, bf16[80,9,2,128]{3,2,1,0:T(2,128)(2,1)S(1)}, u32[]{:S(2)}, u32[]{:S(2)}) %collective-permute-start.14) | collective-permute-done | bytes 368672 | tf_op jit(solution)/shard_map/ppermute | solution.py:249
  95.3 5.1 %collective-permute-done.15 = bf16[80,9,2,128]{3,2,1,0:T(2,128)(2,1)S(1)} collective-permute-done((bf16[80,9,2,128]{3,2,1,0:T(2,128)(2,1)S(1)}, bf16[80,9,2,128]{3,2,1,0:T(2,128)(2,1)S(1)}, u32[]{:S(2)}, u32[]{:S(2)}) %collective-permute-start.15) | collective-permute-done | bytes 368672 | tf_op jit(solution)/shard_map/ppermute | solution.py:249
  100.4 4.0 %collective-permute-start.20 = (bf16[80,9,2,128]{3,2,1,0:T(2,128)(2,1)S(1)}, bf16[80,9,2,128]{3,2,1,0:T(2,128)(2,1)S(1)}, u32[]{:S(2)}, u32[]{:S(2)}) collective-permute-start(bf16[80,9,2,128]{3,2,1,0:T(2,128)(2,1)S(1)} %copy-done.35), channel_id=1, source_target_pairs={{0,10},{1,11},{2,12},{3,13},{4,14},{5,15},{6,8},{7,9},{8,18},{9,19... | collective-permute-start | bytes 1105928 | tf_op jit(solution)/shard_map/ppermute | solution.py:249
  104.4 10.5 %collective-permute-start.21 = (bf16[80,9,2,128]{3,2,1,0:T(2,128)(2,1)}, bf16[80,9,2,128]{3,2,1,0:T(2,128)(2,1)}, u32[]{:S(2)}, u32[]{:S(2)}) collective-permute-start(bf16[80,9,2,128]{3,2,1,0:T(2,128)(2,1)} %get-tuple-element.107), channel_id=1, source_target_pairs={{0,11},{1,10},{2,13},{3,12},{4,15},{5,14},{6,9},{7,8},{8,19},{9,18... | collective-permute-start | bytes 1105928 | tf_op jit(solution)/shard_map/ppermute | solution.py:249
  115.0 6.0 %collective-permute-start.22 = (bf16[80,9,2,128]{3,2,1,0:T(2,128)(2,1)}, bf16[80,9,2,128]{3,2,1,0:T(2,128)(2,1)}, u32[]{:S(2)}, u32[]{:S(2)}) collective-permute-start(bf16[80,9,2,128]{3,2,1,0:T(2,128)(2,1)} %get-tuple-element.108), channel_id=1, source_target_pairs={{0,6},{1,7},{2,0},{3,1},{4,2},{5,3},{6,4},{7,5},{8,14},{9,15},{10,... | collective-permute-start | bytes 1105928 | tf_op jit(solution)/shard_map/ppermute | solution.py:249
  124.4 5.0 %collective-permute-done.21 = bf16[80,9,2,128]{3,2,1,0:T(2,128)(2,1)} collective-permute-done((bf16[80,9,2,128]{3,2,1,0:T(2,128)(2,1)}, bf16[80,9,2,128]{3,2,1,0:T(2,128)(2,1)}, u32[]{:S(2)}, u32[]{:S(2)}) %collective-permute-start.21) | collective-permute-done | bytes 368672 | tf_op jit(solution)/shard_map/ppermute | solution.py:249
  129.4 8.2 %collective-permute-start.29 = (bf16[80,9,2,128]{3,2,1,0:T(2,128)(2,1)S(1)}, bf16[80,9,2,128]{3,2,1,0:T(2,128)(2,1)}, u32[]{:S(2)}, u32[]{:S(2)}) collective-permute-start(bf16[80,9,2,128]{3,2,1,0:T(2,128)(2,1)S(1)} %copy-done.5), channel_id=1, source_target_pairs={{0,9},{1,8},{2,11},{3,10},{4,13},{5,12},{6,15},{7,14},{8,17},{9,16... | collective-permute-start | bytes 1105928 | tf_op jit(solution)/shard_map/ppermute | solution.py:249
  139.8 5.8 %collective-permute-start.28 = (bf16[80,9,2,128]{3,2,1,0:T(2,128)(2,1)}, bf16[80,9,2,128]{3,2,1,0:T(2,128)(2,1)}, u32[]{:S(2)}, u32[]{:S(2)}) collective-permute-start(bf16[80,9,2,128]{3,2,1,0:T(2,128)(2,1)} %get-tuple-element.113), channel_id=1, source_target_pairs={{0,8},{1,9},{2,10},{3,11},{4,12},{5,13},{6,14},{7,15},{8,16},{9,17... | collective-permute-start | bytes 1105928 | tf_op jit(solution)/shard_map/ppermute | solution.py:249
  149.4 8.7 %collective-permute-start = (bf16[80,9,2,128]{3,2,1,0:T(2,128)(2,1)}, bf16[80,9,2,128]{3,2,1,0:T(2,128)(2,1)S(1)}, u32[]{:S(2)}, u32[]{:S(2)}) collective-permute-start(bf16[80,9,2,128]{3,2,1,0:T(2,128)(2,1)} %get-tuple-element.88), channel_id=1, source_target_pairs={{0,20},{1,21},{2,22},{3,23},{4,16},{5,17},{6,18},{7,19},{8,28},{9,... | collective-permute-start | bytes 1105928 | tf_op jit(solution)/shard_map/ppermute | solution.py:249
  159.9 17.3 %collective-permute-start.2 = (bf16[80,9,2,128]{3,2,1,0:T(2,128)(2,1)}, bf16[80,9,2,128]{3,2,1,0:T(2,128)(2,1)S(1)}, u32[]{:S(2)}, u32[]{:S(2)}) collective-permute-start(bf16[80,9,2,128]{3,2,1,0:T(2,128)(2,1)} %get-tuple-element.90), channel_id=1, source_target_pairs={{0,28},{1,29},{2,30},{3,31},{4,24},{5,25},{6,26},{7,27},{8,4},{9,5... | collective-permute-start | bytes 1105928 | tf_op jit(solution)/shard_map/ppermute | solution.py:249
  177.2 4.1 %collective-permute-start.5 = (bf16[80,9,2,128]{3,2,1,0:T(2,128)(2,1)}, bf16[80,9,2,128]{3,2,1,0:T(2,128)(2,1)S(1)}, u32[]{:S(2)}, u32[]{:S(2)}) collective-permute-start(bf16[80,9,2,128]{3,2,1,0:T(2,128)(2,1)} %get-tuple-element.93), channel_id=1, source_target_pairs={{0,13},{1,12},{2,15},{3,14},{4,9},{5,8},{6,11},{7,10},{8,21},{9,20... | collective-permute-start | bytes 1105928 | tf_op jit(solution)/shard_map/ppermute | solution.py:249
  192.7 2.6 %serve.20 = (bf16[2,20736,128]{2,1,0:T(8,128)(2,1)}, bf16[2,2304,128]{2,1,0:T(8,128)(2,1)}, f32[32,256]{1,0:T(8,128)S(1)}) custom-call(bf16[168,144]{1,0:T(8,128)(2,1)S(1)} %copy-done.2, bf16[2,152,72]{2,1,0:T(8,128)(2,1)S(1)} %copy-done.3, bf16[1440,128]{1,0:T(8,128)(2,1)} %bitcast.32.same, ...), custom_call_target="tpu_custom_call", output_to_operand_aliasing={{0}: (4, {}), {1}: (5, {})} | custom-call | flops 123863040 | bytes 3145728 | tf_op jit(solution)/shard_map/serve/pallas_call | solution.py:205
  197.9 2.6 %serve.22 = (bf16[2,20736,128]{2,1,0:T(8,128)(2,1)}, bf16[2,2304,128]{2,1,0:T(8,128)(2,1)}, f32[32,256]{1,0:T(8,128)S(1)}) custom-call(bf16[168,144]{1,0:T(8,128)(2,1)S(1)} %copy-done.2, bf16[2,152,72]{2,1,0:T(8,128)(2,1)S(1)} %copy-done.3, bf16[1440,128]{1,0:T(8,128)(2,1)} %bitcast.84, ...), custom_call_target="tpu_custom_call", output_to_operand_aliasing={{0}: (4, {}), {1}: (5, {})} | custom-call | flops 123863040 | bytes 3145728 | tf_op jit(solution)/shard_map/serve/pallas_call | solution.py:205
  200.5 2.6 %serve.23 = (bf16[2,20736,128]{2,1,0:T(8,128)(2,1)}, bf16[2,2304,128]{2,1,0:T(8,128)(2,1)}, f32[32,256]{1,0:T(8,128)S(1)}) custom-call(bf16[168,144]{1,0:T(8,128)(2,1)S(1)} %copy-done.2, bf16[2,152,72]{2,1,0:T(8,128)(2,1)S(1)} %copy-done.3, bf16[1440,128]{1,0:T(8,128)(2,1)} %bitcast.82, ...), custom_call_target="tpu_custom_call", output_to_operand_aliasing={{0}: (4, {}), {1}: (5, {})} | custom-call | flops 123863040 | bytes 3145728 | tf_op jit(solution)/shard_map/serve/pallas_call | solution.py:205
  208.3 2.6 %serve.26 = (bf16[2,20736,128]{2,1,0:T(8,128)(2,1)}, bf16[2,2304,128]{2,1,0:T(8,128)(2,1)}, f32[32,256]{1,0:T(8,128)S(1)}) custom-call(bf16[168,144]{1,0:T(8,128)(2,1)S(1)} %copy-done.2, bf16[2,152,72]{2,1,0:T(8,128)(2,1)S(1)} %copy-done.3, bf16[1440,128]{1,0:T(8,128)(2,1)} %bitcast.76, ...), custom_call_target="tpu_custom_call", output_to_operand_aliasing={{0}: (4, {}), {1}: (5, {})} | custom-call | flops 123863040 | bytes 3145728 | tf_op jit(solution)/shard_map/serve/pallas_call | solution.py:205
  213.4 2.6 %serve.28 = (bf16[2,20736,128]{2,1,0:T(8,128)(2,1)}, bf16[2,2304,128]{2,1,0:T(8,128)(2,1)}, f32[32,256]{1,0:T(8,128)S(1)}) custom-call(bf16[168,144]{1,0:T(8,128)(2,1)S(1)} %copy-done.2, bf16[2,152,72]{2,1,0:T(8,128)(2,1)S(1)} %copy-done.3, bf16[1440,128]{1,0:T(8,128)(2,1)} %bitcast.72, ...), custom_call_target="tpu_custom_call", output_to_operand_aliasing={{0}: (4, {}), {1}: (5, {})} | custom-call | flops 123863040 | bytes 3145728 | tf_op jit(solution)/shard_map/serve/pallas_call | solution.py:205
  226.5 4.0 %collective-permute-start.31 = (f32[32,2]{0,1:T(2,128)S(1)}, f32[32,2]{0,1:T(2,128)S(1)}, u32[]{:S(2)}, u32[]{:S(2)}) collective-permute-start(f32[32,2]{0,1:T(2,128)S(1)} %copy.51), channel_id=1, source_target_pairs={{0,64},{32,96},{64,0},{96,32},{1,65},{33,97},{65,1},{97,33},{2,66}... | collective-permute-start | bytes 776 | tf_op jit(solution)/shard_map/ppermute | solution.py:262
  (162 shorter events, 69.1 us)
Async XLA Ops:
  24.4 14.2 %collective-permute-start.4 = (bf16[80,9,2,128]{3,2,1,0:T(2,128)(2,1)}, bf16[80,9,2,128]{3,2,1,0:T(2,128)(2,1)S(1)}, u32[]{:S(2)}, u32[]{:S(2)}) collective-permute-start(bf16[80,9,2,128]{3,2,1,0:T(2,128)(2,1)} %get-tuple-element.92), channel_id=1, source_target_pairs={{0,12},{1,13},{2,14},{3,15},{4,8},{5,9},{6,10},{7,11},{8,20},{9,21... | collective-permute-start | bytes 1105928 | tf_op jit(solution)/shard_map/ppermute | solution.py:249
  28.3 21.4 %collective-permute-start.6 = (bf16[80,9,2,128]{3,2,1,0:T(2,128)(2,1)}, bf16[80,9,2,128]{3,2,1,0:T(2,128)(2,1)S(1)}, u32[]{:S(2)}, u32[]{:S(2)}) collective-permute-start(bf16[80,9,2,128]{3,2,1,0:T(2,128)(2,1)} %get-tuple-element.94), channel_id=1, source_target_pairs={{0,22},{1,23},{2,16},{3,17},{4,18},{5,19},{6,20},{7,21},{8,30},{9,... | collective-permute-start | bytes 1105928 | tf_op jit(solution)/shard_map/ppermute | solution.py:249
  29.6 26.1 %collective-permute-start.7 = (bf16[80,9,2,128]{3,2,1,0:T(2,128)(2,1)}, bf16[80,9,2,128]{3,2,1,0:T(2,128)(2,1)S(1)}, u32[]{:S(2)}, u32[]{:S(2)}) collective-permute-start(bf16[80,9,2,128]{3,2,1,0:T(2,128)(2,1)} %get-tuple-element.95), channel_id=1, source_target_pairs={{0,23},{1,22},{2,17},{3,16},{4,19},{5,18},{6,21},{7,20},{8,31},{9,... | collective-permute-start | bytes 1105928 | tf_op jit(solution)/shard_map/ppermute | solution.py:249
  30.5 37.2 %collective-permute-start.8 = (bf16[80,9,2,128]{3,2,1,0:T(2,128)(2,1)}, bf16[80,9,2,128]{3,2,1,0:T(2,128)(2,1)S(1)}, u32[]{:S(2)}, u32[]{:S(2)}) collective-permute-start(bf16[80,9,2,128]{3,2,1,0:T(2,128)(2,1)} %get-tuple-element.96), channel_id=1, source_target_pairs={{0,18},{1,19},{2,20},{3,21},{4,22},{5,23},{6,16},{7,17},{8,26},{9,... | collective-permute-start | bytes 1105928 | tf_op jit(solution)/shard_map/ppermute | solution.py:249
  32.9 43.0 %collective-permute-start.9 = (bf16[80,9,2,128]{3,2,1,0:T(2,128)(2,1)}, bf16[80,9,2,128]{3,2,1,0:T(2,128)(2,1)S(1)}, u32[]{:S(2)}, u32[]{:S(2)}) collective-permute-start(bf16[80,9,2,128]{3,2,1,0:T(2,128)(2,1)} %get-tuple-element.97), channel_id=1, source_target_pairs={{0,19},{1,18},{2,21},{3,20},{4,23},{5,22},{6,17},{7,16},{8,27},{9,... | collective-permute-start | bytes 1105928 | tf_op jit(solution)/shard_map/ppermute | solution.py:249
  38.6 37.4 %collective-permute-start.10 = (bf16[80,9,2,128]{3,2,1,0:T(2,128)(2,1)S(1)}, bf16[80,9,2,128]{3,2,1,0:T(2,128)(2,1)S(1)}, u32[]{:S(2)}, u32[]{:S(2)}) collective-permute-start(bf16[80,9,2,128]{3,2,1,0:T(2,128)(2,1)S(1)} %copy-done.43), channel_id=1, source_target_pairs={{0,4},{1,5},{2,6},{3,7},{4,0},{5,1},{6,2},{7,3},{8,12},{9,13},{10,... | collective-permute-start | bytes 1105928 | tf_op jit(solution)/shard_map/ppermute | solution.py:249
  49.8 31.3 %collective-permute-start.11 = (bf16[80,9,2,128]{3,2,1,0:T(2,128)(2,1)S(1)}, bf16[80,9,2,128]{3,2,1,0:T(2,128)(2,1)S(1)}, u32[]{:S(2)}, u32[]{:S(2)}) collective-permute-start(bf16[80,9,2,128]{3,2,1,0:T(2,128)(2,1)S(1)} %copy-done.10), channel_id=1, source_target_pairs={{0,5},{1,4},{2,7},{3,6},{4,1},{5,0},{6,3},{7,2},{8,13},{9,12},{10,... | collective-permute-start | bytes 1105928 | tf_op jit(solution)/shard_map/ppermute | solution.py:249
  55.7 26.4 %collective-permute-start.12 = (bf16[80,9,2,128]{3,2,1,0:T(2,128)(2,1)S(1)}, bf16[80,9,2,128]{3,2,1,0:T(2,128)(2,1)S(1)}, u32[]{:S(2)}, u32[]{:S(2)}) collective-permute-start(bf16[80,9,2,128]{3,2,1,0:T(2,128)(2,1)S(1)} %copy-done.42), channel_id=1, source_target_pairs={{0,16},{1,17},{2,18},{3,19},{4,20},{5,21},{6,22},{7,23},{8,24},{9,... | collective-permute-start | bytes 1105928 | tf_op jit(solution)/shard_map/ppermute | solution.py:249
  67.7 19.6 %collective-permute-start.13 = (bf16[80,9,2,128]{3,2,1,0:T(2,128)(2,1)S(1)}, bf16[80,9,2,128]{3,2,1,0:T(2,128)(2,1)S(1)}, u32[]{:S(2)}, u32[]{:S(2)}) collective-permute-start(bf16[80,9,2,128]{3,2,1,0:T(2,128)(2,1)S(1)} %copy-done.41), channel_id=1, source_target_pairs={{0,17},{1,16},{2,19},{3,18},{4,21},{5,20},{6,23},{7,22},{8,25},{9,... | collective-permute-start | bytes 1105928 | tf_op jit(solution)/shard_map/ppermute | solution.py:249
  75.9 19.4 %collective-permute-start.14 = (bf16[80,9,2,128]{3,2,1,0:T(2,128)(2,1)S(1)}, bf16[80,9,2,128]{3,2,1,0:T(2,128)(2,1)S(1)}, u32[]{:S(2)}, u32[]{:S(2)}) collective-permute-start(bf16[80,9,2,128]{3,2,1,0:T(2,128)(2,1)S(1)} %copy-done.40), channel_id=1, source_target_pairs={{0,26},{1,27},{2,28},{3,29},{4,30},{5,31},{6,24},{7,25},{8,2},{9,3... | collective-permute-start | bytes 1105928 | tf_op jit(solution)/shard_map/ppermute | solution.py:249
  76.0 24.4 %collective-permute-start.15 = (bf16[80,9,2,128]{3,2,1,0:T(2,128)(2,1)S(1)}, bf16[80,9,2,128]{3,2,1,0:T(2,128)(2,1)S(1)}, u32[]{:S(2)}, u32[]{:S(2)}) collective-permute-start(bf16[80,9,2,128]{3,2,1,0:T(2,128)(2,1)S(1)} %copy-done.39), channel_id=1, source_target_pairs={{0,27},{1,26},{2,29},{3,28},{4,31},{5,30},{6,25},{7,24},{8,3},{9,2... | collective-permute-start | bytes 1105928 | tf_op jit(solution)/shard_map/ppermute | solution.py:249
  81.0 23.4 %collective-permute-start.16 = (bf16[80,9,2,128]{3,2,1,0:T(2,128)(2,1)S(1)}, bf16[80,9,2,128]{3,2,1,0:T(2,128)(2,1)S(1)}, u32[]{:S(2)}, u32[]{:S(2)}) collective-permute-start(bf16[80,9,2,128]{3,2,1,0:T(2,128)(2,1)S(1)} %copy-done.38), channel_id=1, source_target_pairs={{0,14},{1,15},{2,8},{3,9},{4,10},{5,11},{6,12},{7,13},{8,22},{9,23... | collective-permute-start | bytes 1105928 | tf_op jit(solution)/shard_map/ppermute | solution.py:249
  82.1 32.9 %collective-permute-start.17 = (bf16[80,9,2,128]{3,2,1,0:T(2,128)(2,1)S(1)}, bf16[80,9,2,128]{3,2,1,0:T(2,128)(2,1)S(1)}, u32[]{:S(2)}, u32[]{:S(2)}) collective-permute-start(bf16[80,9,2,128]{3,2,1,0:T(2,128)(2,1)S(1)} %copy-done.37), channel_id=1, source_target_pairs={{0,15},{1,14},{2,9},{3,8},{4,11},{5,10},{6,13},{7,12},{8,23},{9,22... | collective-permute-start | bytes 1105928 | tf_op jit(solution)/shard_map/ppermute | solution.py:249
  87.3 33.6 %collective-permute-start.18 = (bf16[80,9,2,128]{3,2,1,0:T(2,128)(2,1)S(1)}, bf16[80,9,2,128]{3,2,1,0:T(2,128)(2,1)S(1)}, u32[]{:S(2)}, u32[]{:S(2)}) collective-permute-start(bf16[80,9,2,128]{3,2,1,0:T(2,128)(2,1)S(1)} %copy-done.36), channel_id=1, source_target_pairs={{0,30},{1,31},{2,24},{3,25},{4,26},{5,27},{6,28},{7,29},{8,6},{9,7... | collective-permute-start | bytes 1105928 | tf_op jit(solution)/shard_map/ppermute | solution.py:249
  95.3 27.4 %collective-permute-start.19 = (bf16[80,9,2,128]{3,2,1,0:T(2,128)(2,1)S(1)}, bf16[80,9,2,128]{3,2,1,0:T(2,128)(2,1)S(1)}, u32[]{:S(2)}, u32[]{:S(2)}) collective-permute-start(bf16[80,9,2,128]{3,2,1,0:T(2,128)(2,1)S(1)} %copy-done.9), channel_id=1, source_target_pairs={{0,31},{1,30},{2,25},{3,24},{4,27},{5,26},{6,29},{7,28},{8,7},{9,6... | collective-permute-start | bytes 1105928 | tf_op jit(solution)/shard_map/ppermute | solution.py:249
  100.4 22.4 %collective-permute-start.20 = (bf16[80,9,2,128]{3,2,1,0:T(2,128)(2,1)S(1)}, bf16[80,9,2,128]{3,2,1,0:T(2,128)(2,1)S(1)}, u32[]{:S(2)}, u32[]{:S(2)}) collective-permute-start(bf16[80,9,2,128]{3,2,1,0:T(2,128)(2,1)S(1)} %copy-done.35), channel_id=1, source_target_pairs={{0,10},{1,11},{2,12},{3,13},{4,14},{5,15},{6,8},{7,9},{8,18},{9,19... | collective-permute-start | bytes 1105928 | tf_op jit(solution)/shard_map/ppermute | solution.py:249
  104.4 25.0 %collective-permute-start.21 = (bf16[80,9,2,128]{3,2,1,0:T(2,128)(2,1)}, bf16[80,9,2,128]{3,2,1,0:T(2,128)(2,1)}, u32[]{:S(2)}, u32[]{:S(2)}) collective-permute-start(bf16[80,9,2,128]{3,2,1,0:T(2,128)(2,1)} %get-tuple-element.107), channel_id=1, source_target_pairs={{0,11},{1,10},{2,13},{3,12},{4,15},{5,14},{6,9},{7,8},{8,19},{9,18... | collective-permute-start | bytes 1105928 | tf_op jit(solution)/shard_map/ppermute | solution.py:249
  115.0 22.7 %collective-permute-start.22 = (bf16[80,9,2,128]{3,2,1,0:T(2,128)(2,1)}, bf16[80,9,2,128]{3,2,1,0:T(2,128)(2,1)}, u32[]{:S(2)}, u32[]{:S(2)}) collective-permute-start(bf16[80,9,2,128]{3,2,1,0:T(2,128)(2,1)} %get-tuple-element.108), channel_id=1, source_target_pairs={{0,6},{1,7},{2,0},{3,1},{4,2},{5,3},{6,4},{7,5},{8,14},{9,15},{10,... | collective-permute-start | bytes 1105928 | tf_op jit(solution)/shard_map/ppermute | solution.py:249
  121.0 16.7 %collective-permute-start.23 = (bf16[80,9,2,128]{3,2,1,0:T(2,128)(2,1)}, bf16[80,9,2,128]{3,2,1,0:T(2,128)(2,1)}, u32[]{:S(2)}, u32[]{:S(2)}) collective-permute-start(bf16[80,9,2,128]{3,2,1,0:T(2,128)(2,1)} %get-tuple-element.109), channel_id=1, source_target_pairs={{0,7},{1,6},{2,1},{3,0},{4,3},{5,2},{6,5},{7,4},{8,15},{9,14},{10,... | collective-permute-start | bytes 1105928 | tf_op jit(solution)/shard_map/ppermute | solution.py:249
  122.8 17.0 %collective-permute-start.24 = (bf16[80,9,2,128]{3,2,1,0:T(2,128)(2,1)}, bf16[80,9,2,128]{3,2,1,0:T(2,128)(2,1)}, u32[]{:S(2)}, u32[]{:S(2)}) collective-permute-start(bf16[80,9,2,128]{3,2,1,0:T(2,128)(2,1)} %get-tuple-element.110), channel_id=1, source_target_pairs={{0,2},{1,3},{2,4},{3,5},{4,6},{5,7},{6,0},{7,1},{8,10},{9,11},{10,... | collective-permute-start | bytes 1105928 | tf_op jit(solution)/shard_map/ppermute | solution.py:249
  122.8 22.9 %collective-permute-start.25 = (bf16[80,9,2,128]{3,2,1,0:T(2,128)(2,1)S(1)}, bf16[80,9,2,128]{3,2,1,0:T(2,128)(2,1)}, u32[]{:S(2)}, u32[]{:S(2)}) collective-permute-start(bf16[80,9,2,128]{3,2,1,0:T(2,128)(2,1)S(1)} %copy-done.7), channel_id=1, source_target_pairs={{0,3},{1,2},{2,5},{3,4},{4,7},{5,6},{6,1},{7,0},{8,11},{9,10},{10,... | collective-permute-start | bytes 1105928 | tf_op jit(solution)/shard_map/ppermute | solution.py:249
  129.4 47.7 %collective-permute-start.29 = (bf16[80,9,2,128]{3,2,1,0:T(2,128)(2,1)S(1)}, bf16[80,9,2,128]{3,2,1,0:T(2,128)(2,1)}, u32[]{:S(2)}, u32[]{:S(2)}) collective-permute-start(bf16[80,9,2,128]{3,2,1,0:T(2,128)(2,1)S(1)} %copy-done.5), channel_id=1, source_target_pairs={{0,9},{1,8},{2,11},{3,10},{4,13},{5,12},{6,15},{7,14},{8,17},{9,16... | collective-permute-start | bytes 1105928 | tf_op jit(solution)/shard_map/ppermute | solution.py:249
  137.6 11.8 %collective-permute-start.26 = (bf16[80,9,2,128]{3,2,1,0:T(2,128)(2,1)}, bf16[80,9,2,128]{3,2,1,0:T(2,128)(2,1)}, u32[]{:S(2)}, u32[]{:S(2)}) collective-permute-start(bf16[80,9,2,128]{3,2,1,0:T(2,128)(2,1)} %get-tuple-element.111), channel_id=1, source_target_pairs={{0,24},{1,25},{2,26},{3,27},{4,28},{5,29},{6,30},{7,31},{8,0},{9,1... | collective-permute-start | bytes 1105928 | tf_op jit(solution)/shard_map/ppermute | solution.py:249
  137.6 20.4 %collective-permute-start.27 = (bf16[80,9,2,128]{3,2,1,0:T(2,128)(2,1)}, bf16[80,9,2,128]{3,2,1,0:T(2,128)(2,1)}, u32[]{:S(2)}, u32[]{:S(2)}) collective-permute-start(bf16[80,9,2,128]{3,2,1,0:T(2,128)(2,1)} %get-tuple-element.112), channel_id=1, source_target_pairs={{0,25},{1,24},{2,27},{3,26},{4,29},{5,28},{6,31},{7,30},{8,1},{9,0... | collective-permute-start | bytes 1105928 | tf_op jit(solution)/shard_map/ppermute | solution.py:249
  139.8 20.1 %collective-permute-start.28 = (bf16[80,9,2,128]{3,2,1,0:T(2,128)(2,1)}, bf16[80,9,2,128]{3,2,1,0:T(2,128)(2,1)}, u32[]{:S(2)}, u32[]{:S(2)}) collective-permute-start(bf16[80,9,2,128]{3,2,1,0:T(2,128)(2,1)} %get-tuple-element.113), channel_id=1, source_target_pairs={{0,8},{1,9},{2,10},{3,11},{4,12},{5,13},{6,14},{7,15},{8,16},{9,17... | collective-permute-start | bytes 1105928 | tf_op jit(solution)/shard_map/ppermute | solution.py:249
  145.6 31.6 %collective-permute-start.30 = (bf16[80,9,2,128]{3,2,1,0:T(2,128)(2,1)}, bf16[80,9,2,128]{3,2,1,0:T(2,128)(2,1)}, u32[]{:S(2)}, u32[]{:S(2)}) collective-permute-start(bf16[80,9,2,128]{3,2,1,0:T(2,128)(2,1)} %get-tuple-element.115), channel_id=1, source_target_pairs={{0,1},{1,0},{2,3},{3,2},{4,5},{5,4},{6,7},{7,6},{8,9},{9,8},{10,11... | collective-permute-start | bytes 1105928 | tf_op jit(solution)/shard_map/ppermute | solution.py:249
  149.4 73.4 %collective-permute-start = (bf16[80,9,2,128]{3,2,1,0:T(2,128)(2,1)}, bf16[80,9,2,128]{3,2,1,0:T(2,128)(2,1)S(1)}, u32[]{:S(2)}, u32[]{:S(2)}) collective-permute-start(bf16[80,9,2,128]{3,2,1,0:T(2,128)(2,1)} %get-tuple-element.88), channel_id=1, source_target_pairs={{0,20},{1,21},{2,22},{3,23},{4,16},{5,17},{6,18},{7,19},{8,28},{9,... | collective-permute-start | bytes 1105928 | tf_op jit(solution)/shard_map/ppermute | solution.py:249
  158.1 64.8 %collective-permute-start.1 = (bf16[80,9,2,128]{3,2,1,0:T(2,128)(2,1)}, bf16[80,9,2,128]{3,2,1,0:T(2,128)(2,1)S(1)}, u32[]{:S(2)}, u32[]{:S(2)}) collective-permute-start(bf16[80,9,2,128]{3,2,1,0:T(2,128)(2,1)} %get-tuple-element.89), channel_id=1, source_target_pairs={{0,21},{1,20},{2,23},{3,22},{4,17},{5,16},{6,19},{7,18},{8,29},{9,... | collective-permute-start | bytes 1105928 | tf_op jit(solution)/shard_map/ppermute | solution.py:249
  159.9 59.5 %collective-permute-start.2 = (bf16[80,9,2,128]{3,2,1,0:T(2,128)(2,1)}, bf16[80,9,2,128]{3,2,1,0:T(2,128)(2,1)S(1)}, u32[]{:S(2)}, u32[]{:S(2)}) collective-permute-start(bf16[80,9,2,128]{3,2,1,0:T(2,128)(2,1)} %get-tuple-element.90), channel_id=1, source_target_pairs={{0,28},{1,29},{2,30},{3,31},{4,24},{5,25},{6,26},{7,27},{8,4},{9,5... | collective-permute-start | bytes 1105928 | tf_op jit(solution)/shard_map/ppermute | solution.py:249
  177.1 42.3 %collective-permute-start.3 = (bf16[80,9,2,128]{3,2,1,0:T(2,128)(2,1)}, bf16[80,9,2,128]{3,2,1,0:T(2,128)(2,1)S(1)}, u32[]{:S(2)}, u32[]{:S(2)}) collective-permute-start(bf16[80,9,2,128]{3,2,1,0:T(2,128)(2,1)} %get-tuple-element.91), channel_id=1, source_target_pairs={{0,29},{1,28},{2,31},{3,30},{4,25},{5,24},{6,27},{7,26},{8,5},{9,4... | collective-permute-start | bytes 1105928 | tf_op jit(solution)/shard_map/ppermute | solution.py:249
  177.2 38.9 %collective-permute-start.5 = (bf16[80,9,2,128]{3,2,1,0:T(2,128)(2,1)}, bf16[80,9,2,128]{3,2,1,0:T(2,128)(2,1)S(1)}, u32[]{:S(2)}, u32[]{:S(2)}) collective-permute-start(bf16[80,9,2,128]{3,2,1,0:T(2,128)(2,1)} %get-tuple-element.93), channel_id=1, source_target_pairs={{0,13},{1,12},{2,15},{3,14},{4,9},{5,8},{6,11},{7,10},{8,21},{9,20... | collective-permute-start | bytes 1105928 | tf_op jit(solution)/shard_map/ppermute | solution.py:249
  226.5 5.6 %collective-permute-start.31 = (f32[32,2]{0,1:T(2,128)S(1)}, f32[32,2]{0,1:T(2,128)S(1)}, u32[]{:S(2)}, u32[]{:S(2)}) collective-permute-start(f32[32,2]{0,1:T(2,128)S(1)} %copy.51), channel_id=1, source_target_pairs={{0,64},{32,96},{64,0},{96,32},{1,65},{33,97},{65,1},{97,33},{2,66}... | collective-permute-start | bytes 776 | tf_op jit(solution)/shard_map/ppermute | solution.py:262
  (45 other events, 2348.3 us)

commit v2 on v1

--- a/solution.py
+++ b/solution.py
@@ -11,16 +11,20 @@
 
 HEAD_DIM = 128
 FF = 36864
-STORED = 46
-BLK = 128
 NHEAD = 64
 
 stored_unit = 1.0 / 1024.0
 
-ORDER = [(1, 0), (3, 0), (0, 1), (0, 3), (1, 1), (3, 3), (1, 3), (3, 1), (2, 0), (0, 2), (2, 1), (2, 3), (1, 2), (3, 2), (2, 2)]
-
-MOVES = [(dx, dy, dc) for dx, dy in ORDER for dc in (0, 1)] + [(0, 0, 1), (0, 0, 0)]
-COUNTS = [2, 4, 6, 8, 12]
+RINGS = [
+    [(1, 1), (3, 3), (1, 3), (3, 1)],
+    [(2, 2)],
+    [(1, 0), (3, 0), (0, 1), (0, 3)],
+    [(2, 0), (0, 2)],
+    [(2, 1), (2, 3), (1, 2), (3, 2)],
+]
+MOVES = [(dx, dy, dc) for ring in RINGS for dc in (0, 1) for dx, dy in ring] + [(0, 0, 1), (0, 0, 0)]
+SERVED = [(0, 0)] + [move[:2] for move in MOVES[:-2] if move[2] == 1]
+COUNTS = [4, 6, 6, 8, 8]
 
 ROWS = 36
 TILES = FF // 32 // 128
@@ -45,64 +49,48 @@
     return pltpu.with_memory_space_constraint(x, pltpu.HBM)
 
 
-def in_vmem(x):
-    return pltpu.with_memory_space_constraint(x, pltpu.VMEM)
-
-
 def here():
     me = lax.axis_index("dev")
     return lax.div(me, 8), lax.rem(lax.div(me, 2), 4), lax.rem(me, 2)
 
 
 def cut_kernel(shifts, heads, gate, qkv, *rest):
-    outs, (held, in_sems, out_sems) = rest[-3 - len(shifts) : -3], rest[-3:]
+    outs, sems = rest[-1 - len(shifts) : -1], rest[-1]
     x, y, c = here()
-    loads = []
-    for i, (dx, dy, dc) in enumerate(shifts):
+    copies = []
+    for i, ((dx, dy, dc), out) in enumerate(zip(shifts, outs)):
         owner = (lax.rem(x + dx, 4) * 4 + lax.rem(y + dy, 4)) * 2 + lax.rem(c + dc, 2)
-        loads.append(
-            [
+        for p in range(2):
+            copies.append(
                 pltpu.make_async_copy(
                     gate.at[:, pl.ds(p * 32 * TILES + owner * TILES, TILES)],
-                    held.at[i, pl.ds(p * ROWS, ROWS)],
-                    in_sems.at[i, p],
+                    out.at[pl.ds(p * ROWS, ROWS)],
+                    sems.at[i, p],
                 )
-                for p in range(2)
-            ]
-            + [
+            )
+        for k in range(2):
+            copies.append(
                 pltpu.make_async_copy(
                     qkv.at[:, :, heads[2 * owner + k]],
-                    held.at[i, pl.ds(2 * ROWS + 4 * k, 4)],
-                    in_sems.at[i, 2 + k],
+                    out.at[pl.ds(2 * ROWS + 4 * k, 4)],
+                    sems.at[i, 2 + k],
                 )
-                for k in range(2)
-            ]
-        )
-    stores = [pltpu.make_async_copy(held.at[i], out, out_sems.at[i]) for i, out in enumerate(outs)]
-    for load in loads:
-        for copy in load:
-            copy.start()
-    for load, store in zip(loads, stores):
-        for copy in load:
-            copy.wait()
-        store.start()
-    for store in stores:
-        store.wait()
+            )
+    for copy in copies:
+        copy.start()
+    for copy in copies:
+        copy.wait()
 
 
 def cut(shifts, heads, gate, qkv, after):
     size = int(np.prod(PIECE)) * 2 * len(shifts)
     return pl.pallas_call(
         functools.partial(cut_kernel, shifts),
-        out_shape=[pltpu.HBM(PIECE, jnp.bfloat16)] * len(shifts),
+        out_shape=[pltpu.VMEM(PIECE, jnp.bfloat16)] * len(shifts),
         in_specs=[pl.BlockSpec(memory_space=pltpu.SMEM)] + [pl.BlockSpec(memory_space=pl.ANY)] * (2 + len(after)),
         out_specs=[pl.BlockSpec(memory_space=pl.ANY)] * len(shifts),
-        scratch_shapes=[
-            pltpu.VMEM((len(shifts), *PIECE), jnp.bfloat16),
-            pltpu.SemaphoreType.DMA((len(shifts), 4)),
-            pltpu.SemaphoreType.DMA((len(shifts),)),
-        ],
-        compiler_params=pltpu.CompilerParams(vmem_limit_bytes=(len(shifts) + 1) << 19),
+        scratch_shapes=[pltpu.SemaphoreType.DMA((len(shifts), 4))],
+        compiler_params=pltpu.CompilerParams(vmem_limit_bytes=1 << 20),
         cost_estimate=pl.CostEstimate(flops=size, bytes_accessed=2 * size, transcendentals=0),
         name="cut",
     )(heads, gate, qkv, *after)
@@ -157,6 +145,7 @@
         return jnp.dot(a, b, preferred_element_type=jnp.float32)
 
     gate_sum = jnp.zeros((24, 256), jnp.float32)
+    copies = []
     for g in range(9):
         if g < 4:
             got = dot(turn[...], both(0, 144 * g, 144))
@@ -168,6 +157,14 @@
             for p in range(2):
                 gate_buf[l, pl.ds(144 * g + 72 * p, 72), :] = got[l * 72 : (l + 1) * 72, p * 128 : (p + 1) * 128].astype(jnp.bfloat16)
         gate_sum += got[144:168]
+        copies.append(
+            pltpu.make_async_copy(
+                gate_buf.at[:, pl.ds(144 * g, 144)],
+                gate_out.at[:, pl.ds(pl.multiple_of(chip * 1296 + 144 * g, 16), 144)],
+                out_sems.at[g],
+            )
+        )
+        copies[-1].start()
     got = None
     for part in range(2):
         heads = jnp.concatenate([held_heads[part, pl.ds(72 * k, 72)] for k in range(2)], axis=1)
@@ -183,13 +180,11 @@
         head_sum = head_sum + sums_in[24:32, :]
     sums[0:24, :] = gate_sum
     sums[24:32, :] = head_sum
-    out = [
-        pltpu.make_async_copy(gate_buf, gate_out.at[:, pl.ds(pl.multiple_of(chip * 1296, 16), 1296)], out_sems.at[0]),
-        pltpu.make_async_copy(qkv_buf, qkv_out.at[:, pl.ds(pl.multiple_of(chip * 144, 16), 144)], out_sems.at[1]),
-    ]
-    for copy in out:
-        copy.start()
-    for copy in out:
+    copies.append(
+        pltpu.make_async_copy(qkv_buf, qkv_out.at[:, pl.ds(pl.multiple_of(chip * 144, 16), 144)], out_sems.at[9])
+    )
+    copies[-1].start()
+    for copy in copies:
         copy.wait()
 
 
@@ -201,7 +196,6 @@
     if first:
         kernel = lambda a, b, c, d, *rest: serve_kernel(shift, a, b, c, d, None, None, None, *rest)
     pieces = [same.reshape(1440, 128), other.reshape(1440, 128)]
-    pieces = [in_hbm(piece) for piece in pieces]
     return pl.pallas_call(
         kernel,
         out_shape=[
@@ -217,7 +211,7 @@
             pltpu.VMEM((2, 1296, 128), jnp.bfloat16),
             pltpu.VMEM((2, 144, 128), jnp.bfloat16),
             pltpu.SemaphoreType.DMA((2, 3)),
-            pltpu.SemaphoreType.DMA((2,)),
+            pltpu.SemaphoreType.DMA((10,)),
         ],
         input_output_aliases={} if first else {4: 0, 5: 1},
         compiler_params=pltpu.CompilerParams(vmem_limit_bytes=8 << 20),
@@ -226,17 +220,95 @@
     )(turn, head_turn, *pieces, *(() if first else done))
 
 
+def picks():
+    gate = np.zeros((24, GATE_ROWS), np.float32)
+    for k in range(GATE_ROWS):
+        gate[(k % 2) * TILES + k // 2 % TILES, k] = 1
+    head = np.zeros((8, HEAD_ROWS), np.float32)
+    for k in range(HEAD_ROWS):
+        head[k % 2, k] = 1
+    return jnp.asarray(gate, jnp.bfloat16), jnp.asarray(head, jnp.bfloat16)
+
+
+def tally_kernel(gate, head, before, same, other, out):
+    for p in range(2):
+        lanes = slice(128 * p, 128 * (p + 1))
+        gates, heads = before[0:24, lanes], before[24:32, lanes]
+        for piece in (same, other):
+            rows = piece[pl.ds(GATE_ROWS * p, GATE_ROWS)]
+            gates += jnp.dot(gate[...], rows, preferred_element_type=jnp.float32)
+            rows = piece[pl.ds(2 * GATE_ROWS + HEAD_ROWS * p, HEAD_ROWS)]
+            heads += jnp.dot(head[...], rows, preferred_element_type=jnp.float32)
+        out[0:24, lanes] = gates
+        out[24:32, lanes] = heads
+
+
+def tally(before, pieces):
+    vmem_spec = pl.BlockSpec(memory_space=pltpu.VMEM)
+    return pl.pallas_call(
+        tally_kernel,
+        out_shape=pltpu.VMEM((32, 256), jnp.float32),
+        in_specs=[vmem_spec] * 5,
+        out_specs=vmem_spec,
+        compiler_params=pltpu.CompilerParams(vmem_limit_bytes=4 << 20),
+        name="tally",
+    )(*picks(), before, *[piece.reshape(1440, 128) for piece in pieces])
+
+
+def pick_kernel(heads, layer_ids, stored_qkv, stored_gate, gate_pick, qkv_pick):
+    owner = lax.axis_index("dev")
+
+    def table(width, value):
+        row = lax.broadcasted_iota(jnp.int32, (2, width), 0)
+        column = lax.broadcasted_iota(jnp.int32, (2, width), 1)
+        out = jnp.zeros((2, width), jnp.int32)
+        for l in range(2):
+            for b in range(width):
+                out = jnp.where((row == l) & (column == b), value(layer_ids[l], b), out)
+        return out.astype(jnp.float32) * stored_unit
+
+    gate_pick[...] = table(18, lambda l, b: stored_gate[l, (b // TILES) * 32 * TILES + owner * TILES + b % TILES])
+    qkv_pick[...] = table(2, lambda l, b: stored_qkv[l, heads[2 * owner + b]])
+
+
+def pick(heads, layer_ids, stored_qkv, stored_gate):
+    return pl.pallas_call(
+        pick_kernel,
+        out_shape=[pltpu.VMEM((2, 18), jnp.float32), pltpu.VMEM((2, 2), jnp.float32)],
+        in_specs=[pl.BlockSpec(memory_space=pltpu.SMEM)] * 4,
+        out_specs=[pl.BlockSpec(memory_space=pltpu.VMEM)] * 2,
+        compiler_params=pltpu.CompilerParams(vmem_limit_bytes=1 << 20),
+        name="pick",
+    )(heads, layer_ids, stored_qkv, stored_gate)
+
+
+def settle_kernel(a, b, c, d, gate_pick, qkv_pick, gate_out, qkv_out):
+    total = (a[...] + b[...] + c[...] + d[...]).T
+    sums = [jnp.sum(total[128 * p : 128 * (p + 1)], axis=0, keepdims=True) for p in range(2)]
+    for l in range(2):
+        row = jnp.concatenate([s[:, TILES * l : TILES * (l + 1)] for s in sums], axis=1)
+        gate_out[l : l + 1, :] = row - gate_pick[l : l + 1, :]
+        row = jnp.concatenate([s[:, 24 + l : 25 + l] for s in sums], axis=1)
+        qkv_out[l : l + 1, :] = row - qkv_pick[l : l + 1, :]
+
+
+def settle(totals, gate_pick, qkv_pick):
+    return pl.pallas_call(
+        settle_kernel,
+        out_shape=[jax.ShapeDtypeStruct((2, 18), jnp.float32), jax.ShapeDtypeStruct((2, 2), jnp.float32)],
+        in_specs=[pl.BlockSpec(memory_space=pltpu.VMEM)] * 6,
+        out_specs=[pl.BlockSpec(memory_space=pltpu.VMEM)] * 2,
+        compiler_params=pltpu.CompilerParams(vmem_limit_bytes=1 << 20),
+        name="settle",
+    )(*totals, gate_pick, qkv_pick)
+
+
 def relayout(qkv_weight, gate_up_weight, head_slot, layer_ids, stored_qkv, stored_gate_up):
-    owners = lax.axis_size("dev")
-    owner = lax.axis_index("dev")
-    layers = qkv_weight.shape[0]
-    slots = NHEAD // owners
-    blocks = FF // owners // BLK
     gate = gate_up_weight.transpose(1, 0, 2).reshape(ROWS, 2, 2 * FF // 128, 128).transpose(0, 2, 1, 3)
     qkv = qkv_weight.transpose(1, 0, 2).reshape(4, 9, 2, NHEAD, HEAD_DIM).transpose(0, 1, 3, 2, 4)
 
     moves = MOVES
-    gate, qkv = in_hbm(gate), in_vmem(qkv)
+    gate, qkv = in_hbm(gate), in_hbm(qkv)
     pieces = {}
     at, after = 0, ()
     for count in COUNTS:
@@ -251,27 +323,18 @@
 
     turn, head_turn = turns()
     done = None
-    for shift in [(0, 0)] + ORDER:
+    for i, shift in enumerate(SERVED):
+        if i == len(SERVED) - 1:
+            totals = [tally(done[2], [got[(*shift, dc)] for dc in (0, 1)])]
+            for step in (1, 2, 3):
+                totals.append(lax.ppermute(totals[0], "grp", [(g, (g + step) % 4) for g in range(4)]))
         done = serve(shift, turn, head_turn, got[(*shift, 0)], got[(*shift, 1)], done)
-    gate_out, qkv_out, total = done
+    gate_out, qkv_out = done[:2]
     served_qkv = qkv_out.reshape(2, 144, 2, 8, 128).transpose(0, 1, 3, 2, 4).reshape(2, 1152, 256)
     served_gate = gate_out.reshape(2, 144, 18, 8, 128).transpose(0, 1, 3, 2, 4).reshape(2, 1152, 2304)
 
-    lane = jnp.sum(total.reshape(32, 2, 128), axis=2)
-    for step in (2, 1):
-        lane = lane + lax.ppermute(lane, "grp", [(g, g ^ step) for g in range(4)])
-    block_sum = lane[:18].reshape(2, 9, 2).transpose(0, 2, 1).reshape(2, 18)
-    head_sum = lane[24:26]
-
-    layer_pick = (layer_ids[:, None] == jnp.arange(STORED, dtype=jnp.int32)[None, :]).astype(jnp.float32)
-    picked_qkv = jnp.dot(layer_pick, stored_qkv.astype(jnp.float32), precision=lax.Precision.HIGHEST, preferred_element_type=jnp.float32)
-    picked_gate = jnp.dot(layer_pick, stored_gate_up.astype(jnp.float32), precision=lax.Precision.HIGHEST, preferred_element_type=jnp.float32)
-    own_heads = lax.dynamic_slice_in_dim(head_slot, owner * slots, slots, 0)
-    picked_qkv = picked_qkv[:, own_heads]
-    picked_gate = picked_gate.reshape(layers, 2, owners, blocks).transpose(0, 2, 1, 3).reshape(layers, owners * 2 * blocks)
-    picked_gate = lax.dynamic_slice_in_dim(picked_gate, owner * 2 * blocks, 2 * blocks, 1)
-    qkv_mismatch = head_sum - picked_qkv * stored_unit
-    gate_up_mismatch = block_sum - picked_gate * stored_unit
+    gate_pick, qkv_pick = pick(head_slot, layer_ids, stored_qkv, stored_gate_up)
+    gate_up_mismatch, qkv_mismatch = settle(totals, gate_pick, qkv_pick)
     return served_qkv, served_gate, qkv_mismatch, gate_up_mismatch
 
 

time: 238 us -> 189 us (0.79)
  the two profiles are of different devices: /device:TPU:4 before, /device:TPU:40 now
where the time goes in v2:
time: 189 us; the launch traced here: 188 us
  starting transfers between devices  78.9 us (42%)
  waiting for transfers between devices  54.3 us (29%)
  Pallas kernels  53.1 us (28%)
    ppermute x31, starting transfers between devices, relayout(): got[move] = lax.ppermute(pieces[move], 'dev', moved_pairs(*move))  73.3 us
    ppermute x31, waiting for transfers between devices, relayout(): got[move] = lax.ppermute(pieces[move], 'dev', moved_pairs(*move))  54.3 us
    pallas_call x16, Pallas kernels, serve(): pl.pallas_call(kernel, out_shape=[pltpu.HBM((2, 16 * 1296, 128), jnp.bflo...  36.2 us
    pallas_call x5, Pallas kernels, cut(): pl.pallas_call(functools.partial(cut_kernel, shifts), out_shape=[pltpu.VM...  12.8 us
    ppermute x3, starting transfers between devices, relayout(): lax.ppermute(totals[0], 'grp', [(g, (g + step) % 4) for g in range(4)])  5.68 us
  transfers between devices with their start and end apart: 34, of which 13 were waited for; matrix products, arithmetic and copies ran while one was open for 0% of the time, Pallas kernels for 22%

profile of v2, /device:TPU:40, one launch (start us, length us, event | category | flops | bytes accessed | tf_op | source)
XLA Modules:
  0.0 188.0 jit_solution(7169709942203054964)
XLA Ops:
  3.5 2.5 %cut.6 = (bf16[80,9,2,128]{3,2,1,0:T(2,128)(2,1)S(1)}, bf16[80,9,2,128]{3,2,1,0:T(2,128)(2,1)S(1)}, bf16[80,9,2,128]{3,2,1,0:T(2,128)(2,1)S(1)}, bf16[80,9,2,128...) custom-call(s32[64]{0:T(128)S(1)} %copy-done.5, ...), custom_call_target="tpu_custom_call" | custom-call | flops 2211840 | bytes 4423680 | tf_op jit(solution)/shard_map/cut/pallas_call | solution.py:87
  6.0 2.5 %cut.7 = (bf16[80,9,2,128]{3,2,1,0:T(2,128)(2,1)S(1)}, bf16[80,9,2,128]{3,2,1,0:T(2,128)(2,1)S(1)}, bf16[80,9,2,128]{3,2,1,0:T(2,128)(2,1)S(1)}, bf16[80,9,2,128...) custom-call(s32[64]{0:T(128)S(1)} %copy-done.5, ...), custom_call_target="tpu_custom_call" | custom-call | flops 2211840 | bytes 4423680 | tf_op jit(solution)/shard_map/cut/pallas_call | solution.py:87
  8.5 2.8 %cut.8 = (bf16[80,9,2,128]{3,2,1,0:T(2,128)(2,1)S(1)}, bf16[80,9,2,128]{3,2,1,0:T(2,128)(2,1)S(1)}, bf16[80,9,2,128]{3,2,1,0:T(2,128)(2,1)S(1)}, bf16[80,9,2,128...) custom-call(s32[64]{0:T(128)S(1)} %copy-done.5, ...), custom_call_target="tpu_custom_call" | custom-call | flops 2949120 | bytes 5898240 | tf_op jit(solution)/shard_map/cut/pallas_call | solution.py:87
  11.3 3.0 %collective-permute-start.4 = (bf16[80,9,2,128]{3,2,1,0:T(2,128)(2,1)S(1)}, bf16[80,9,2,128]{3,2,1,0:T(2,128)(2,1)S(1)}, u32[]{:S(2)}, u32[]{:S(2)}) collective-permute-start(bf16[80,9,2,128]{3,2,1,0:T(2,128)(2,1)S(1)} %get-tuple-element.90.rest_0_), channel_id=1, source_target_pairs={{0,22},{1,23},{2,16},{3,17},{4,18},{5,19},{6,20},{7,21},{8,30},{9,... | collective-permute-start | bytes 1105928 | tf_op jit(solution)/shard_map/ppermute | solution.py:321
  15.8 2.8 %cut.9 = (bf16[80,9,2,128]{3,2,1,0:T(2,128)(2,1)S(1)}, bf16[80,9,2,128]{3,2,1,0:T(2,128)(2,1)S(1)}, bf16[80,9,2,128]{3,2,1,0:T(2,128)(2,1)S(1)}, bf16[80,9,2,128...) custom-call(s32[64]{0:T(128)S(1)} %copy-done.6, ...), custom_call_target="tpu_custom_call" | custom-call | flops 2949120 | bytes 5898240 | tf_op jit(solution)/shard_map/cut/pallas_call | solution.py:87
  18.6 3.0 %collective-permute-start.7 = (bf16[80,9,2,128]{3,2,1,0:T(2,128)(2,1)S(1)}, bf16[80,9,2,128]{3,2,1,0:T(2,128)(2,1)S(1)}, u32[]{:S(2)}, u32[]{:S(2)}) collective-permute-start(bf16[80,9,2,128]{3,2,1,0:T(2,128)(2,1)S(1)} %get-tuple-element.97), channel_id=1, source_target_pairs={{0,19},{1,18},{2,21},{3,20},{4,23},{5,22},{6,17},{7,16},{8,27},{9,... | collective-permute-start | bytes 1105928 | tf_op jit(solution)/shard_map/ppermute | solution.py:321
  22.6 3.1 %collective-permute-start.9 = (bf16[80,9,2,128]{3,2,1,0:T(2,128)(2,1)S(1)}, bf16[80,9,2,128]{3,2,1,0:T(2,128)(2,1)S(1)}, u32[]{:S(2)}, u32[]{:S(2)}) collective-permute-start(bf16[80,9,2,128]{3,2,1,0:T(2,128)(2,1)S(1)} %get-tuple-element.99), channel_id=1, source_target_pairs={{0,5},{1,4},{2,7},{3,6},{4,1},{5,0},{6,3},{7,2},{8,13},{9,12},{10,... | collective-permute-start | bytes 1105928 | tf_op jit(solution)/shard_map/ppermute | solution.py:321
  25.7 2.6 %collective-permute-start.10 = (bf16[80,9,2,128]{3,2,1,0:T(2,128)(2,1)S(1)}, bf16[80,9,2,128]{3,2,1,0:T(2,128)(2,1)S(1)}, u32[]{:S(2)}, u32[]{:S(2)}) collective-permute-start(bf16[80,9,2,128]{3,2,1,0:T(2,128)(2,1)S(1)} %get-tuple-element.100), channel_id=1, source_target_pairs={{0,16},{1,17},{2,18},{3,19},{4,20},{5,21},{6,22},{7,23},{8,24},{9,... | collective-permute-start | bytes 1105928 | tf_op jit(solution)/shard_map/ppermute | solution.py:321
  28.3 6.4 %collective-permute-done.6 = bf16[80,9,2,128]{3,2,1,0:T(2,128)(2,1)S(1)} collective-permute-done((bf16[80,9,2,128]{3,2,1,0:T(2,128)(2,1)S(1)}, bf16[80,9,2,128]{3,2,1,0:T(2,128)(2,1)S(1)}, u32[]{:S(2)}, u32[]{:S(2)}) %collective-permute-start.6) | collective-permute-done | bytes 368672 | tf_op jit(solution)/shard_map/ppermute | solution.py:321
  35.1 5.3 %collective-permute-done.7 = bf16[80,9,2,128]{3,2,1,0:T(2,128)(2,1)S(1)} collective-permute-done((bf16[80,9,2,128]{3,2,1,0:T(2,128)(2,1)S(1)}, bf16[80,9,2,128]{3,2,1,0:T(2,128)(2,1)S(1)}, u32[]{:S(2)}, u32[]{:S(2)}) %collective-permute-start.7) | collective-permute-done | bytes 368672 | tf_op jit(solution)/shard_map/ppermute | solution.py:321
  42.1 7.6 %collective-permute-start.13 = (bf16[80,9,2,128]{3,2,1,0:T(2,128)(2,1)S(1)}, bf16[80,9,2,128]{3,2,1,0:T(2,128)(2,1)S(1)}, u32[]{:S(2)}, u32[]{:S(2)}) collective-permute-start(bf16[80,9,2,128]{3,2,1,0:T(2,128)(2,1)S(1)} %get-tuple-element.103), channel_id=1, source_target_pairs={{0,7},{1,6},{2,1},{3,0},{4,3},{5,2},{6,5},{7,4},{8,15},{9,14},{10,... | collective-permute-start | bytes 1105928 | tf_op jit(solution)/shard_map/ppermute | solution.py:321
  49.7 8.9 %collective-permute-start.14 = (bf16[80,9,2,128]{3,2,1,0:T(2,128)(2,1)S(1)}, bf16[80,9,2,128]{3,2,1,0:T(2,128)(2,1)S(1)}, u32[]{:S(2)}, u32[]{:S(2)}) collective-permute-start(bf16[80,9,2,128]{3,2,1,0:T(2,128)(2,1)S(1)} %get-tuple-element.104), channel_id=1, source_target_pairs={{0,2},{1,3},{2,4},{3,5},{4,6},{5,7},{6,0},{7,1},{8,10},{9,11},{10,... | collective-permute-start | bytes 1105928 | tf_op jit(solution)/shard_map/ppermute | solution.py:321
  58.6 2.5 %collective-permute-start.16 = (bf16[80,9,2,128]{3,2,1,0:T(2,128)(2,1)S(1)}, bf16[80,9,2,128]{3,2,1,0:T(2,128)(2,1)S(1)}, u32[]{:S(2)}, u32[]{:S(2)}) collective-permute-start(bf16[80,9,2,128]{3,2,1,0:T(2,128)(2,1)S(1)} %get-tuple-element.106), channel_id=1, source_target_pairs={{0,24},{1,25},{2,26},{3,27},{4,28},{5,29},{6,30},{7,31},{8,0},{9,1... | collective-permute-start | bytes 1105928 | tf_op jit(solution)/shard_map/ppermute | solution.py:321
  62.6 5.0 %collective-permute-done.14 = bf16[80,9,2,128]{3,2,1,0:T(2,128)(2,1)S(1)} collective-permute-done((bf16[80,9,2,128]{3,2,1,0:T(2,128)(2,1)S(1)}, bf16[80,9,2,128]{3,2,1,0:T(2,128)(2,1)S(1)}, u32[]{:S(2)}, u32[]{:S(2)}) %collective-permute-start.14) | collective-permute-done | bytes 368672 | tf_op jit(solution)/shard_map/ppermute | solution.py:321
  67.6 7.0 %collective-permute-done.15 = bf16[80,9,2,128]{3,2,1,0:T(2,128)(2,1)S(1)} collective-permute-done((bf16[80,9,2,128]{3,2,1,0:T(2,128)(2,1)S(1)}, bf16[80,9,2,128]{3,2,1,0:T(2,128)(2,1)S(1)}, u32[]{:S(2)}, u32[]{:S(2)}) %collective-permute-start.15) | collective-permute-done | bytes 368672 | tf_op jit(solution)/shard_map/ppermute | solution.py:321
  74.6 3.1 %collective-permute-start.20 = (bf16[80,9,2,128]{3,2,1,0:T(2,128)(2,1)S(1)}, bf16[80,9,2,128]{3,2,1,0:T(2,128)(2,1)S(1)}, u32[]{:S(2)}, u32[]{:S(2)}) collective-permute-start(bf16[80,9,2,128]{3,2,1,0:T(2,128)(2,1)S(1)} %get-tuple-element.109), channel_id=1, source_target_pairs={{0,20},{1,21},{2,22},{3,23},{4,16},{5,17},{6,18},{7,19},{8,28},{9,... | collective-permute-start | bytes 1105928 | tf_op jit(solution)/shard_map/ppermute | solution.py:321
  79.9 4.3 %collective-permute-start.22 = (bf16[80,9,2,128]{3,2,1,0:T(2,128)(2,1)S(1)}, bf16[80,9,2,128]{3,2,1,0:T(2,128)(2,1)S(1)}, u32[]{:S(2)}, u32[]{:S(2)}) collective-permute-start(bf16[80,9,2,128]{3,2,1,0:T(2,128)(2,1)S(1)} %get-tuple-element.87.rest_0_), channel_id=1, source_target_pairs={{0,26},{1,27},{2,28},{3,29},{4,30},{5,31},{6,24},{7,25},{8,2},{9,3... | collective-permute-start | bytes 1105928 | tf_op jit(solution)/shard_map/ppermute | solution.py:321
  86.2 3.9 %collective-permute-done.20 = bf16[80,9,2,128]{3,2,1,0:T(2,128)(2,1)S(1)} collective-permute-done((bf16[80,9,2,128]{3,2,1,0:T(2,128)(2,1)S(1)}, bf16[80,9,2,128]{3,2,1,0:T(2,128)(2,1)S(1)}, u32[]{:S(2)}, u32[]{:S(2)}) %collective-permute-start.20) | collective-permute-done | bytes 368672 | tf_op jit(solution)/shard_map/ppermute | solution.py:321
  91.8 4.6 %collective-permute-done.21 = bf16[80,9,2,128]{3,2,1,0:T(2,128)(2,1)S(1)} collective-permute-done((bf16[80,9,2,128]{3,2,1,0:T(2,128)(2,1)S(1)}, bf16[80,9,2,128]{3,2,1,0:T(2,128)(2,1)S(1)}, u32[]{:S(2)}, u32[]{:S(2)}) %collective-permute-start.21) | collective-permute-done | bytes 368672 | tf_op jit(solution)/shard_map/ppermute | solution.py:321
  96.4 6.8 %collective-permute-start.26 = (bf16[80,9,2,128]{3,2,1,0:T(2,128)(2,1)S(1)}, bf16[80,9,2,128]{3,2,1,0:T(2,128)(2,1)S(1)}, u32[]{:S(2)}, u32[]{:S(2)}) collective-permute-start(bf16[80,9,2,128]{3,2,1,0:T(2,128)(2,1)S(1)} %get-tuple-element.113), channel_id=1, source_target_pairs={{0,30},{1,31},{2,24},{3,25},{4,26},{5,27},{6,28},{7,29},{8,6},{9,7... | collective-permute-start | bytes 1105928 | tf_op jit(solution)/shard_map/ppermute | solution.py:321
  103.2 2.9 %collective-permute-done.22 = bf16[80,9,2,128]{3,2,1,0:T(2,128)(2,1)S(1)} collective-permute-done((bf16[80,9,2,128]{3,2,1,0:T(2,128)(2,1)S(1)}, bf16[80,9,2,128]{3,2,1,0:T(2,128)(2,1)S(1)}, u32[]{:S(2)}, u32[]{:S(2)}) %collective-permute-start.22) | collective-permute-done | bytes 368672 | tf_op jit(solution)/shard_map/ppermute | solution.py:321
  106.1 2.3 %collective-permute-start.27 = (bf16[80,9,2,128]{3,2,1,0:T(2,128)(2,1)S(1)}, bf16[80,9,2,128]{3,2,1,0:T(2,128)(2,1)S(1)}, u32[]{:S(2)}, u32[]{:S(2)}) collective-permute-start(bf16[80,9,2,128]{3,2,1,0:T(2,128)(2,1)S(1)} %get-tuple-element.114), channel_id=1, source_target_pairs={{0,31},{1,30},{2,25},{3,24},{4,27},{5,26},{6,29},{7,28},{8,7},{9,6... | collective-permute-start | bytes 1105928 | tf_op jit(solution)/shard_map/ppermute | solution.py:321
  108.4 5.8 %collective-permute-done.23 = bf16[80,9,2,128]{3,2,1,0:T(2,128)(2,1)S(1)} collective-permute-done((bf16[80,9,2,128]{3,2,1,0:T(2,128)(2,1)S(1)}, bf16[80,9,2,128]{3,2,1,0:T(2,128)(2,1)S(1)}, u32[]{:S(2)}, u32[]{:S(2)}) %collective-permute-start.23) | collective-permute-done | bytes 368672 | tf_op jit(solution)/shard_map/ppermute | solution.py:321
  116.7 5.0 %collective-permute-done.26 = bf16[80,9,2,128]{3,2,1,0:T(2,128)(2,1)S(1)} collective-permute-done((bf16[80,9,2,128]{3,2,1,0:T(2,128)(2,1)S(1)}, bf16[80,9,2,128]{3,2,1,0:T(2,128)(2,1)S(1)}, u32[]{:S(2)}, u32[]{:S(2)}) %collective-permute-start.26) | collective-permute-done | bytes 368672 | tf_op jit(solution)/shard_map/ppermute | solution.py:321
  121.7 2.5 %collective-permute-start.5 = (bf16[80,9,2,128]{3,2,1,0:T(2,128)(2,1)S(1)}, bf16[80,9,2,128]{3,2,1,0:T(2,128)(2,1)S(1)}, u32[]{:S(2)}, u32[]{:S(2)}) collective-permute-start(bf16[80,9,2,128]{3,2,1,0:T(2,128)(2,1)S(1)} %get-tuple-element.95), channel_id=1, source_target_pairs={{0,23},{1,22},{2,17},{3,16},{4,19},{5,18},{6,21},{7,20},{8,31},{9,... | collective-permute-start | bytes 1105928 | tf_op jit(solution)/shard_map/ppermute | solution.py:321
  124.2 6.0 %collective-permute-done.27 = bf16[80,9,2,128]{3,2,1,0:T(2,128)(2,1)S(1)} collective-permute-done((bf16[80,9,2,128]{3,2,1,0:T(2,128)(2,1)S(1)}, bf16[80,9,2,128]{3,2,1,0:T(2,128)(2,1)S(1)}, u32[]{:S(2)}, u32[]{:S(2)}) %collective-permute-start.27) | collective-permute-done | bytes 368672 | tf_op jit(solution)/shard_map/ppermute | solution.py:321
  130.2 2.8 %collective-permute-start.2 = (bf16[80,9,2,128]{3,2,1,0:T(2,128)(2,1)S(1)}, bf16[80,9,2,128]{3,2,1,0:T(2,128)(2,1)S(1)}, u32[]{:S(2)}, u32[]{:S(2)}) collective-permute-start(bf16[80,9,2,128]{3,2,1,0:T(2,128)(2,1)S(1)} %get-tuple-element.93), channel_id=1, source_target_pairs={{0,12},{1,13},{2,14},{3,15},{4,8},{5,9},{6,10},{7,11},{8,20},{9,21... | collective-permute-start | bytes 1105928 | tf_op jit(solution)/shard_map/ppermute | solution.py:321
  133.5 4.6 %collective-permute-start = (bf16[80,9,2,128]{3,2,1,0:T(2,128)(2,1)S(1)}, bf16[80,9,2,128]{3,2,1,0:T(2,128)(2,1)S(1)}, u32[]{:S(2)}, u32[]{:S(2)}) collective-permute-start(bf16[80,9,2,128]{3,2,1,0:T(2,128)(2,1)S(1)} %get-tuple-element.91), channel_id=1, source_target_pairs={{0,28},{1,29},{2,30},{3,31},{4,24},{5,25},{6,26},{7,27},{8,4},{9,5... | collective-permute-start | bytes 1105928 | tf_op jit(solution)/shard_map/ppermute | solution.py:321
  168.9 2.2 %serve.29 = (bf16[2,20736,128]{2,1,0:T(8,128)(2,1)}, bf16[2,2304,128]{2,1,0:T(8,128)(2,1)}, f32[32,256]{1,0:T(8,128)S(1)}) custom-call(bf16[168,144]{1,0:T(8,128)(2,1)S(1)} %copy-done, bf16[2,152,72]{2,1,0:T(8,128)(2,1)S(1)} %copy-done.1, bf16[1440,128]{1,0:T(8,128)(2,1)S(1)} %bitcast.56, ...), custom_call_target="tpu_custom_call", output_to_operand_aliasing={{0}: (4, {}), {1}: (5, {})} | custom-call | flops 123863040 | bytes 3145728 | tf_op jit(solution)/shard_map/serve/pallas_call | solution.py:199
  178.8 2.5 %collective-permute-start.33 = (f32[32,256]{1,0:T(8,128)S(1)}, f32[32,256]{1,0:T(8,128)S(1)}, u32[]{:S(2)}, u32[]{:S(2)}) collective-permute-start(f32[32,256]{1,0:T(8,128)S(1)} %tally.1.a), channel_id=1, source_target_pairs={{0,96},{32,0},{64,32},{96,64},{1,97},{33,1},{65,33},{97,65},{2,98}... | collective-permute-start | bytes 98312 | tf_op jit(solution)/shard_map/ppermute | solution.py:330
  181.3 3.1 %pick.1 = (f32[2,18]{1,0:T(2,128)S(1)}, f32[2,2]{1,0:T(2,128)S(1)}) custom-call(s32[64]{0:T(128)S(1)} %copy-done.6, s32[2]{0:T(128)S(1)} %copy-done.8, s32[46,64]{1,0:T(8,128)S(1)} %copy-done.4, s32[46,576]{1,0:T(8,128)S(1)} %copy-done.2), custom_call_target="tpu_custom_call" | custom-call | tf_op jit(solution)/shard_map/pick/pallas_call | solution.py:275
  184.4 2.8 %serve.31 = (bf16[2,20736,128]{2,1,0:T(8,128)(2,1)}, bf16[2,2304,128]{2,1,0:T(8,128)(2,1)}, f32[32,256]{1,0:T(8,128)}) custom-call(bf16[168,144]{1,0:T(8,128)(2,1)S(1)} %copy-done, bf16[2,152,72]{2,1,0:T(8,128)(2,1)S(1)} %copy-done.1, bf16[1440,128]{1,0:T(8,128)(2,1)S(1)} %bitcast.53, ...), custom_call_target="tpu_custom_call", output_to_operand_aliasing={{0}: (4, {}), {1}: (5, {})} | custom-call | flops 123863040 | bytes 3145728 | tf_op jit(solution)/shard_map/serve/pallas_call | solution.py:199
  (78 shorter events, 56.7 us)
Async XLA Ops:
  11.3 14.4 %collective-permute-start.4 = (bf16[80,9,2,128]{3,2,1,0:T(2,128)(2,1)S(1)}, bf16[80,9,2,128]{3,2,1,0:T(2,128)(2,1)S(1)}, u32[]{:S(2)}, u32[]{:S(2)}) collective-permute-start(bf16[80,9,2,128]{3,2,1,0:T(2,128)(2,1)S(1)} %get-tuple-element.90.rest_0_), channel_id=1, source_target_pairs={{0,22},{1,23},{2,16},{3,17},{4,18},{5,19},{6,20},{7,21},{8,30},{9,... | collective-permute-start | bytes 1105928 | tf_op jit(solution)/shard_map/ppermute | solution.py:321
  14.3 20.4 %collective-permute-start.6 = (bf16[80,9,2,128]{3,2,1,0:T(2,128)(2,1)S(1)}, bf16[80,9,2,128]{3,2,1,0:T(2,128)(2,1)S(1)}, u32[]{:S(2)}, u32[]{:S(2)}) collective-permute-start(bf16[80,9,2,128]{3,2,1,0:T(2,128)(2,1)S(1)} %get-tuple-element.96), channel_id=1, source_target_pairs={{0,18},{1,19},{2,20},{3,21},{4,22},{5,23},{6,16},{7,17},{8,26},{9,... | collective-permute-start | bytes 1105928 | tf_op jit(solution)/shard_map/ppermute | solution.py:321
  18.6 21.7 %collective-permute-start.7 = (bf16[80,9,2,128]{3,2,1,0:T(2,128)(2,1)S(1)}, bf16[80,9,2,128]{3,2,1,0:T(2,128)(2,1)S(1)}, u32[]{:S(2)}, u32[]{:S(2)}) collective-permute-start(bf16[80,9,2,128]{3,2,1,0:T(2,128)(2,1)S(1)} %get-tuple-element.97), channel_id=1, source_target_pairs={{0,19},{1,18},{2,21},{3,20},{4,23},{5,22},{6,17},{7,16},{8,27},{9,... | collective-permute-start | bytes 1105928 | tf_op jit(solution)/shard_map/ppermute | solution.py:321
  21.6 20.5 %collective-permute-start.8 = (bf16[80,9,2,128]{3,2,1,0:T(2,128)(2,1)S(1)}, bf16[80,9,2,128]{3,2,1,0:T(2,128)(2,1)S(1)}, u32[]{:S(2)}, u32[]{:S(2)}) collective-permute-start(bf16[80,9,2,128]{3,2,1,0:T(2,128)(2,1)S(1)} %get-tuple-element.98), channel_id=1, source_target_pairs={{0,4},{1,5},{2,6},{3,7},{4,0},{5,1},{6,2},{7,3},{8,12},{9,13},{10,... | collective-permute-start | bytes 1105928 | tf_op jit(solution)/shard_map/ppermute | solution.py:321
  22.6 27.1 %collective-permute-start.9 = (bf16[80,9,2,128]{3,2,1,0:T(2,128)(2,1)S(1)}, bf16[80,9,2,128]{3,2,1,0:T(2,128)(2,1)S(1)}, u32[]{:S(2)}, u32[]{:S(2)}) collective-permute-start(bf16[80,9,2,128]{3,2,1,0:T(2,128)(2,1)S(1)} %get-tuple-element.99), channel_id=1, source_target_pairs={{0,5},{1,4},{2,7},{3,6},{4,1},{5,0},{6,3},{7,2},{8,13},{9,12},{10,... | collective-permute-start | bytes 1105928 | tf_op jit(solution)/shard_map/ppermute | solution.py:321
  25.7 32.9 %collective-permute-start.10 = (bf16[80,9,2,128]{3,2,1,0:T(2,128)(2,1)S(1)}, bf16[80,9,2,128]{3,2,1,0:T(2,128)(2,1)S(1)}, u32[]{:S(2)}, u32[]{:S(2)}) collective-permute-start(bf16[80,9,2,128]{3,2,1,0:T(2,128)(2,1)S(1)} %get-tuple-element.100), channel_id=1, source_target_pairs={{0,16},{1,17},{2,18},{3,19},{4,20},{5,21},{6,22},{7,23},{8,24},{9,... | collective-permute-start | bytes 1105928 | tf_op jit(solution)/shard_map/ppermute | solution.py:321
  34.7 23.9 %collective-permute-start.11 = (bf16[80,9,2,128]{3,2,1,0:T(2,128)(2,1)S(1)}, bf16[80,9,2,128]{3,2,1,0:T(2,128)(2,1)S(1)}, u32[]{:S(2)}, u32[]{:S(2)}) collective-permute-start(bf16[80,9,2,128]{3,2,1,0:T(2,128)(2,1)S(1)} %get-tuple-element.101), channel_id=1, source_target_pairs={{0,17},{1,16},{2,19},{3,18},{4,21},{5,20},{6,23},{7,22},{8,25},{9,... | collective-permute-start | bytes 1105928 | tf_op jit(solution)/shard_map/ppermute | solution.py:321
  40.3 20.8 %collective-permute-start.12 = (bf16[80,9,2,128]{3,2,1,0:T(2,128)(2,1)S(1)}, bf16[80,9,2,128]{3,2,1,0:T(2,128)(2,1)S(1)}, u32[]{:S(2)}, u32[]{:S(2)}) collective-permute-start(bf16[80,9,2,128]{3,2,1,0:T(2,128)(2,1)S(1)} %get-tuple-element.102), channel_id=1, source_target_pairs={{0,6},{1,7},{2,0},{3,1},{4,2},{5,3},{6,4},{7,5},{8,14},{9,15},{10,... | collective-permute-start | bytes 1105928 | tf_op jit(solution)/shard_map/ppermute | solution.py:321
  42.1 19.1 %collective-permute-start.13 = (bf16[80,9,2,128]{3,2,1,0:T(2,128)(2,1)S(1)}, bf16[80,9,2,128]{3,2,1,0:T(2,128)(2,1)S(1)}, u32[]{:S(2)}, u32[]{:S(2)}) collective-permute-start(bf16[80,9,2,128]{3,2,1,0:T(2,128)(2,1)S(1)} %get-tuple-element.103), channel_id=1, source_target_pairs={{0,7},{1,6},{2,1},{3,0},{4,3},{5,2},{6,5},{7,4},{8,15},{9,14},{10,... | collective-permute-start | bytes 1105928 | tf_op jit(solution)/shard_map/ppermute | solution.py:321
  49.7 17.9 %collective-permute-start.14 = (bf16[80,9,2,128]{3,2,1,0:T(2,128)(2,1)S(1)}, bf16[80,9,2,128]{3,2,1,0:T(2,128)(2,1)S(1)}, u32[]{:S(2)}, u32[]{:S(2)}) collective-permute-start(bf16[80,9,2,128]{3,2,1,0:T(2,128)(2,1)S(1)} %get-tuple-element.104), channel_id=1, source_target_pairs={{0,2},{1,3},{2,4},{3,5},{4,6},{5,7},{6,0},{7,1},{8,10},{9,11},{10,... | collective-permute-start | bytes 1105928 | tf_op jit(solution)/shard_map/ppermute | solution.py:321
  58.6 16.0 %collective-permute-start.15 = (bf16[80,9,2,128]{3,2,1,0:T(2,128)(2,1)S(1)}, bf16[80,9,2,128]{3,2,1,0:T(2,128)(2,1)S(1)}, u32[]{:S(2)}, u32[]{:S(2)}) collective-permute-start(bf16[80,9,2,128]{3,2,1,0:T(2,128)(2,1)S(1)} %get-tuple-element.105), channel_id=1, source_target_pairs={{0,3},{1,2},{2,5},{3,4},{4,7},{5,6},{6,1},{7,0},{8,11},{9,10},{10,... | collective-permute-start | bytes 1105928 | tf_op jit(solution)/shard_map/ppermute | solution.py:321
  58.6 19.1 %collective-permute-start.16 = (bf16[80,9,2,128]{3,2,1,0:T(2,128)(2,1)S(1)}, bf16[80,9,2,128]{3,2,1,0:T(2,128)(2,1)S(1)}, u32[]{:S(2)}, u32[]{:S(2)}) collective-permute-start(bf16[80,9,2,128]{3,2,1,0:T(2,128)(2,1)S(1)} %get-tuple-element.106), channel_id=1, source_target_pairs={{0,24},{1,25},{2,26},{3,27},{4,28},{5,29},{6,30},{7,31},{8,0},{9,1... | collective-permute-start | bytes 1105928 | tf_op jit(solution)/shard_map/ppermute | solution.py:321
  61.2 18.8 %collective-permute-start.17 = (bf16[80,9,2,128]{3,2,1,0:T(2,128)(2,1)S(1)}, bf16[80,9,2,128]{3,2,1,0:T(2,128)(2,1)S(1)}, u32[]{:S(2)}, u32[]{:S(2)}) collective-permute-start(bf16[80,9,2,128]{3,2,1,0:T(2,128)(2,1)S(1)} %get-tuple-element.89.rest_0_), channel_id=1, source_target_pairs={{0,25},{1,24},{2,27},{3,26},{4,29},{5,28},{6,31},{7,30},{8,1},{9,0... | collective-permute-start | bytes 1105928 | tf_op jit(solution)/shard_map/ppermute | solution.py:321
  61.2 23.1 %collective-permute-start.18 = (bf16[80,9,2,128]{3,2,1,0:T(2,128)(2,1)S(1)}, bf16[80,9,2,128]{3,2,1,0:T(2,128)(2,1)S(1)}, u32[]{:S(2)}, u32[]{:S(2)}) collective-permute-start(bf16[80,9,2,128]{3,2,1,0:T(2,128)(2,1)S(1)} %get-tuple-element.107), channel_id=1, source_target_pairs={{0,8},{1,9},{2,10},{3,11},{4,12},{5,13},{6,14},{7,15},{8,16},{9,17... | collective-permute-start | bytes 1105928 | tf_op jit(solution)/shard_map/ppermute | solution.py:321
  67.6 16.7 %collective-permute-start.19 = (bf16[80,9,2,128]{3,2,1,0:T(2,128)(2,1)S(1)}, bf16[80,9,2,128]{3,2,1,0:T(2,128)(2,1)S(1)}, u32[]{:S(2)}, u32[]{:S(2)}) collective-permute-start(bf16[80,9,2,128]{3,2,1,0:T(2,128)(2,1)S(1)} %get-tuple-element.108), channel_id=1, source_target_pairs={{0,9},{1,8},{2,11},{3,10},{4,13},{5,12},{6,15},{7,14},{8,17},{9,16... | collective-permute-start | bytes 1105928 | tf_op jit(solution)/shard_map/ppermute | solution.py:321
  74.6 15.5 %collective-permute-start.20 = (bf16[80,9,2,128]{3,2,1,0:T(2,128)(2,1)S(1)}, bf16[80,9,2,128]{3,2,1,0:T(2,128)(2,1)S(1)}, u32[]{:S(2)}, u32[]{:S(2)}) collective-permute-start(bf16[80,9,2,128]{3,2,1,0:T(2,128)(2,1)S(1)} %get-tuple-element.109), channel_id=1, source_target_pairs={{0,20},{1,21},{2,22},{3,23},{4,16},{5,17},{6,18},{7,19},{8,28},{9,... | collective-permute-start | bytes 1105928 | tf_op jit(solution)/shard_map/ppermute | solution.py:321
  77.7 18.7 %collective-permute-start.21 = (bf16[80,9,2,128]{3,2,1,0:T(2,128)(2,1)S(1)}, bf16[80,9,2,128]{3,2,1,0:T(2,128)(2,1)S(1)}, u32[]{:S(2)}, u32[]{:S(2)}) collective-permute-start(bf16[80,9,2,128]{3,2,1,0:T(2,128)(2,1)S(1)} %get-tuple-element.88.rest_0_), channel_id=1, source_target_pairs={{0,21},{1,20},{2,23},{3,22},{4,17},{5,16},{6,19},{7,18},{8,29},{9,... | collective-permute-start | bytes 1105928 | tf_op jit(solution)/shard_map/ppermute | solution.py:321
  79.9 26.2 %collective-permute-start.22 = (bf16[80,9,2,128]{3,2,1,0:T(2,128)(2,1)S(1)}, bf16[80,9,2,128]{3,2,1,0:T(2,128)(2,1)S(1)}, u32[]{:S(2)}, u32[]{:S(2)}) collective-permute-start(bf16[80,9,2,128]{3,2,1,0:T(2,128)(2,1)S(1)} %get-tuple-element.87.rest_0_), channel_id=1, source_target_pairs={{0,26},{1,27},{2,28},{3,29},{4,30},{5,31},{6,24},{7,25},{8,2},{9,3... | collective-permute-start | bytes 1105928 | tf_op jit(solution)/shard_map/ppermute | solution.py:321
  84.3 30.0 %collective-permute-start.23 = (bf16[80,9,2,128]{3,2,1,0:T(2,128)(2,1)S(1)}, bf16[80,9,2,128]{3,2,1,0:T(2,128)(2,1)S(1)}, u32[]{:S(2)}, u32[]{:S(2)}) collective-permute-start(bf16[80,9,2,128]{3,2,1,0:T(2,128)(2,1)S(1)} %get-tuple-element.110), channel_id=1, source_target_pairs={{0,27},{1,26},{2,29},{3,28},{4,31},{5,30},{6,25},{7,24},{8,3},{9,2... | collective-permute-start | bytes 1105928 | tf_op jit(solution)/shard_map/ppermute | solution.py:321
  84.3 31.9 %collective-permute-start.24 = (bf16[80,9,2,128]{3,2,1,0:T(2,128)(2,1)S(1)}, bf16[80,9,2,128]{3,2,1,0:T(2,128)(2,1)S(1)}, u32[]{:S(2)}, u32[]{:S(2)}) collective-permute-start(bf16[80,9,2,128]{3,2,1,0:T(2,128)(2,1)S(1)} %get-tuple-element.111), channel_id=1, source_target_pairs={{0,14},{1,15},{2,8},{3,9},{4,10},{5,11},{6,12},{7,13},{8,22},{9,23... | collective-permute-start | bytes 1105928 | tf_op jit(solution)/shard_map/ppermute | solution.py:321
  90.1 26.1 %collective-permute-start.25 = (bf16[80,9,2,128]{3,2,1,0:T(2,128)(2,1)S(1)}, bf16[80,9,2,128]{3,2,1,0:T(2,128)(2,1)S(1)}, u32[]{:S(2)}, u32[]{:S(2)}) collective-permute-start(bf16[80,9,2,128]{3,2,1,0:T(2,128)(2,1)S(1)} %get-tuple-element.112), channel_id=1, source_target_pairs={{0,15},{1,14},{2,9},{3,8},{4,11},{5,10},{6,13},{7,12},{8,23},{9,22... | collective-permute-start | bytes 1105928 | tf_op jit(solution)/shard_map/ppermute | solution.py:321
  96.4 25.3 %collective-permute-start.26 = (bf16[80,9,2,128]{3,2,1,0:T(2,128)(2,1)S(1)}, bf16[80,9,2,128]{3,2,1,0:T(2,128)(2,1)S(1)}, u32[]{:S(2)}, u32[]{:S(2)}) collective-permute-start(bf16[80,9,2,128]{3,2,1,0:T(2,128)(2,1)S(1)} %get-tuple-element.113), channel_id=1, source_target_pairs={{0,30},{1,31},{2,24},{3,25},{4,26},{5,27},{6,28},{7,29},{8,6},{9,7... | collective-permute-start | bytes 1105928 | tf_op jit(solution)/shard_map/ppermute | solution.py:321
  106.1 24.1 %collective-permute-start.27 = (bf16[80,9,2,128]{3,2,1,0:T(2,128)(2,1)S(1)}, bf16[80,9,2,128]{3,2,1,0:T(2,128)(2,1)S(1)}, u32[]{:S(2)}, u32[]{:S(2)}) collective-permute-start(bf16[80,9,2,128]{3,2,1,0:T(2,128)(2,1)S(1)} %get-tuple-element.114), channel_id=1, source_target_pairs={{0,31},{1,30},{2,25},{3,24},{4,27},{5,26},{6,29},{7,28},{8,7},{9,6... | collective-permute-start | bytes 1105928 | tf_op jit(solution)/shard_map/ppermute | solution.py:321
  114.3 18.7 %collective-permute-start.28 = (bf16[80,9,2,128]{3,2,1,0:T(2,128)(2,1)S(1)}, bf16[80,9,2,128]{3,2,1,0:T(2,128)(2,1)S(1)}, u32[]{:S(2)}, u32[]{:S(2)}) collective-permute-start(bf16[80,9,2,128]{3,2,1,0:T(2,128)(2,1)S(1)} %get-tuple-element.115), channel_id=1, source_target_pairs={{0,10},{1,11},{2,12},{3,13},{4,14},{5,15},{6,8},{7,9},{8,18},{9,19... | collective-permute-start | bytes 1105928 | tf_op jit(solution)/shard_map/ppermute | solution.py:321
  116.2 17.3 %collective-permute-start.29 = (bf16[80,9,2,128]{3,2,1,0:T(2,128)(2,1)S(1)}, bf16[80,9,2,128]{3,2,1,0:T(2,128)(2,1)S(1)}, u32[]{:S(2)}, u32[]{:S(2)}) collective-permute-start(bf16[80,9,2,128]{3,2,1,0:T(2,128)(2,1)S(1)} %get-tuple-element.116), channel_id=1, source_target_pairs={{0,11},{1,10},{2,13},{3,12},{4,15},{5,14},{6,9},{7,8},{8,19},{9,18... | collective-permute-start | bytes 1105928 | tf_op jit(solution)/shard_map/ppermute | solution.py:321
  116.2 21.8 %collective-permute-start.30 = (bf16[80,9,2,128]{3,2,1,0:T(2,128)(2,1)S(1)}, bf16[80,9,2,128]{3,2,1,0:T(2,128)(2,1)S(1)}, u32[]{:S(2)}, u32[]{:S(2)}) collective-permute-start(bf16[80,9,2,128]{3,2,1,0:T(2,128)(2,1)S(1)} %get-tuple-element.118), channel_id=1, source_target_pairs={{0,1},{1,0},{2,3},{3,2},{4,5},{5,4},{6,7},{7,6},{8,9},{9,8},{10,11... | collective-permute-start | bytes 1105928 | tf_op jit(solution)/shard_map/ppermute | solution.py:321
  121.7 47.1 %collective-permute-start.5 = (bf16[80,9,2,128]{3,2,1,0:T(2,128)(2,1)S(1)}, bf16[80,9,2,128]{3,2,1,0:T(2,128)(2,1)S(1)}, u32[]{:S(2)}, u32[]{:S(2)}) collective-permute-start(bf16[80,9,2,128]{3,2,1,0:T(2,128)(2,1)S(1)} %get-tuple-element.95), channel_id=1, source_target_pairs={{0,23},{1,22},{2,17},{3,16},{4,19},{5,18},{6,21},{7,20},{8,31},{9,... | collective-permute-start | bytes 1105928 | tf_op jit(solution)/shard_map/ppermute | solution.py:321
  130.2 40.9 %collective-permute-start.2 = (bf16[80,9,2,128]{3,2,1,0:T(2,128)(2,1)S(1)}, bf16[80,9,2,128]{3,2,1,0:T(2,128)(2,1)S(1)}, u32[]{:S(2)}, u32[]{:S(2)}) collective-permute-start(bf16[80,9,2,128]{3,2,1,0:T(2,128)(2,1)S(1)} %get-tuple-element.93), channel_id=1, source_target_pairs={{0,12},{1,13},{2,14},{3,15},{4,8},{5,9},{6,10},{7,11},{8,20},{9,21... | collective-permute-start | bytes 1105928 | tf_op jit(solution)/shard_map/ppermute | solution.py:321
  133.0 39.5 %collective-permute-start.3 = (bf16[80,9,2,128]{3,2,1,0:T(2,128)(2,1)S(1)}, bf16[80,9,2,128]{3,2,1,0:T(2,128)(2,1)S(1)}, u32[]{:S(2)}, u32[]{:S(2)}) collective-permute-start(bf16[80,9,2,128]{3,2,1,0:T(2,128)(2,1)S(1)} %get-tuple-element.94), channel_id=1, source_target_pairs={{0,13},{1,12},{2,15},{3,14},{4,9},{5,8},{6,11},{7,10},{8,21},{9,20... | collective-permute-start | bytes 1105928 | tf_op jit(solution)/shard_map/ppermute | solution.py:321
  133.5 41.2 %collective-permute-start = (bf16[80,9,2,128]{3,2,1,0:T(2,128)(2,1)S(1)}, bf16[80,9,2,128]{3,2,1,0:T(2,128)(2,1)S(1)}, u32[]{:S(2)}, u32[]{:S(2)}) collective-permute-start(bf16[80,9,2,128]{3,2,1,0:T(2,128)(2,1)S(1)} %get-tuple-element.91), channel_id=1, source_target_pairs={{0,28},{1,29},{2,30},{3,31},{4,24},{5,25},{6,26},{7,27},{8,4},{9,5... | collective-permute-start | bytes 1105928 | tf_op jit(solution)/shard_map/ppermute | solution.py:321
  138.0 37.3 %collective-permute-start.1 = (bf16[80,9,2,128]{3,2,1,0:T(2,128)(2,1)S(1)}, bf16[80,9,2,128]{3,2,1,0:T(2,128)(2,1)S(1)}, u32[]{:S(2)}, u32[]{:S(2)}) collective-permute-start(bf16[80,9,2,128]{3,2,1,0:T(2,128)(2,1)S(1)} %get-tuple-element.92), channel_id=1, source_target_pairs={{0,29},{1,28},{2,31},{3,30},{4,25},{5,24},{6,27},{7,26},{8,5},{9,4... | collective-permute-start | bytes 1105928 | tf_op jit(solution)/shard_map/ppermute | solution.py:321
  175.6 11.6 %collective-permute-start.31 = (f32[32,256]{1,0:T(8,128)S(1)}, f32[32,256]{1,0:T(8,128)S(1)}, u32[]{:S(2)}, u32[]{:S(2)}) collective-permute-start(f32[32,256]{1,0:T(8,128)S(1)} %tally.1.a), channel_id=1, source_target_pairs={{0,32},{32,64},{64,96},{96,0},{1,33},{33,65},{65,97},{97,1},{2,34}... | collective-permute-start | bytes 98312 | tf_op jit(solution)/shard_map/ppermute | solution.py:330
  (11 other events, 341.4 us)

commit v3 on v2

--- a/solution.py
+++ b/solution.py
@@ -230,11 +230,12 @@
     return jnp.asarray(gate, jnp.bfloat16), jnp.asarray(head, jnp.bfloat16)
 
 
-def tally_kernel(gate, head, before, same, other, out):
+def tally_kernel(gate, head, before, *refs):
+    pieces, out = refs[:-1], refs[-1]
     for p in range(2):
         lanes = slice(128 * p, 128 * (p + 1))
         gates, heads = before[0:24, lanes], before[24:32, lanes]
-        for piece in (same, other):
+        for piece in pieces:
             rows = piece[pl.ds(GATE_ROWS * p, GATE_ROWS)]
             gates += jnp.dot(gate[...], rows, preferred_element_type=jnp.float32)
             rows = piece[pl.ds(2 * GATE_ROWS + HEAD_ROWS * p, HEAD_ROWS)]
@@ -248,11 +249,27 @@
     return pl.pallas_call(
         tally_kernel,
         out_shape=pltpu.VMEM((32, 256), jnp.float32),
-        in_specs=[vmem_spec] * 5,
+        in_specs=[vmem_spec] * (3 + len(pieces)),
         out_specs=vmem_spec,
         compiler_params=pltpu.CompilerParams(vmem_limit_bytes=4 << 20),
         name="tally",
     )(*picks(), before, *[piece.reshape(1440, 128) for piece in pieces])
+
+
+def merge_kernel(a, b, out):
+    out[...] = a[...] + b[...]
+
+
+def merge(a, b):
+    vmem_spec = pl.BlockSpec(memory_space=pltpu.VMEM)
+    return pl.pallas_call(
+        merge_kernel,
+        out_shape=pltpu.VMEM((32, 256), jnp.float32),
+        in_specs=[vmem_spec] * 2,
+        out_specs=vmem_spec,
+        compiler_params=pltpu.CompilerParams(vmem_limit_bytes=1 << 20),
+        name="merge",
+    )(a, b)
 
 
 def pick_kernel(heads, layer_ids, stored_qkv, stored_gate, gate_pick, qkv_pick):
@@ -282,8 +299,8 @@
     )(heads, layer_ids, stored_qkv, stored_gate)
 
 
-def settle_kernel(a, b, c, d, gate_pick, qkv_pick, gate_out, qkv_out):
-    total = (a[...] + b[...] + c[...] + d[...]).T
+def settle_kernel(a, b, gate_pick, qkv_pick, gate_out, qkv_out):
+    total = (a[...] + b[...]).T
     sums = [jnp.sum(total[128 * p : 128 * (p + 1)], axis=0, keepdims=True) for p in range(2)]
     for l in range(2):
         row = jnp.concatenate([s[:, TILES * l : TILES * (l + 1)] for s in sums], axis=1)
@@ -296,7 +313,7 @@
     return pl.pallas_call(
         settle_kernel,
         out_shape=[jax.ShapeDtypeStruct((2, 18), jnp.float32), jax.ShapeDtypeStruct((2, 2), jnp.float32)],
-        in_specs=[pl.BlockSpec(memory_space=pltpu.VMEM)] * 6,
+        in_specs=[pl.BlockSpec(memory_space=pltpu.VMEM)] * 4,
         out_specs=[pl.BlockSpec(memory_space=pltpu.VMEM)] * 2,
         compiler_params=pltpu.CompilerParams(vmem_limit_bytes=1 << 20),
         name="settle",
@@ -323,18 +340,21 @@
 
     turn, head_turn = turns()
     done = None
+    last = len(SERVED) - 1
     for i, shift in enumerate(SERVED):
-        if i == len(SERVED) - 1:
-            totals = [tally(done[2], [got[(*shift, dc)] for dc in (0, 1)])]
-            for step in (1, 2, 3):
-                totals.append(lax.ppermute(totals[0], "grp", [(g, (g + step) % 4) for g in range(4)]))
+        if i == last - 1:
+            mine = tally(done[2], [got[(*late, dc)] for late in SERVED[-2:] for dc in (0, 1)])
+            near = lax.ppermute(mine, "grp", [(0, 1), (1, 0), (2, 3), (3, 2)])
+        if i == last:
+            mine = merge(mine, near)
+            near = lax.ppermute(mine, "grp", [(0, 3), (3, 0), (1, 2), (2, 1)])
         done = serve(shift, turn, head_turn, got[(*shift, 0)], got[(*shift, 1)], done)
     gate_out, qkv_out = done[:2]
     served_qkv = qkv_out.reshape(2, 144, 2, 8, 128).transpose(0, 1, 3, 2, 4).reshape(2, 1152, 256)
     served_gate = gate_out.reshape(2, 144, 18, 8, 128).transpose(0, 1, 3, 2, 4).reshape(2, 1152, 2304)
 
     gate_pick, qkv_pick = pick(head_slot, layer_ids, stored_qkv, stored_gate_up)
-    gate_up_mismatch, qkv_mismatch = settle(totals, gate_pick, qkv_pick)
+    gate_up_mismatch, qkv_mismatch = settle((mine, near), gate_pick, qkv_pick)
     return served_qkv, served_gate, qkv_mismatch, gate_up_mismatch
 
 

time: 189 us -> 193 us (1.021); the launches traced: 188 us -> 190 us
  waiting for transfers between devices: 54.3 us -> 60.6 us
  starting transfers between devices: 78.9 us -> 74.4 us
    ppermute x3 -> x2, waiting for transfers between devices: 0.01 us -> 4.15 us  [the longest x1 4.15 us: relayout(): near = lax.ppermute(mine, 'grp', [(0, 1), (1, 0), (2, 3), (3, 2)])]
    ppermute x3 -> x2, starting transfers between devices: 5.68 us -> 2.1 us  [the longest x1 1.92 us: relayout(): near = lax.ppermute(mine, 'grp', [(0, 3), (3, 0), (1, 2), (2, 1)])]
    ppermute x31, waiting for transfers between devices: 54.3 us -> 56.5 us  [relayout(): got[move] = lax.ppermute(pieces[move], 'dev', moved_pairs(*move))]
  transfers between devices with their start and end apart: 34 -> 33, of which waited for: 13 -> 13; matrix products, arithmetic and copies ran while one was open for 0% -> 0% of each run, Pallas kernels for 22% -> 22%
where the time goes in v3:
time: 193 us; the launch traced here: 190 us
  starting transfers between devices  74.4 us (39%)
  waiting for transfers between devices  60.6 us (31%)
  Pallas kernels  53.3 us (28%)
    ppermute x31, starting transfers between devices, relayout(): got[move] = lax.ppermute(pieces[move], 'dev', moved_pairs(*move))  72.3 us
    ppermute x31, waiting for transfers between devices, relayout(): got[move] = lax.ppermute(pieces[move], 'dev', moved_pairs(*move))  56.5 us
    pallas_call x16, Pallas kernels, serve(): pl.pallas_call(kernel, out_shape=[pltpu.HBM((2, 16 * 1296, 128), jnp.bflo...  36.3 us
    pallas_call x5, Pallas kernels, cut(): pl.pallas_call(functools.partial(cut_kernel, shifts), out_shape=[pltpu.VM...  12.8 us
    ppermute x1, waiting for transfers between devices, relayout(): near = lax.ppermute(mine, 'grp', [(0, 1), (1, 0), (2, 3), (3, 2)])  4.15 us
  transfers between devices with their start and end apart: 33, of which 13 were waited for; matrix products, arithmetic and copies ran while one was open for 0% of the time, Pallas kernels for 22%

profile of v3, /device:TPU:40, one launch (start us, length us, event | category | flops | bytes accessed | tf_op | source)
XLA Modules:
  0.0 189.9 jit_solution(8542251302915134653)
XLA Ops:
  3.5 2.5 %cut.6 = (bf16[80,9,2,128]{3,2,1,0:T(2,128)(2,1)S(1)}, bf16[80,9,2,128]{3,2,1,0:T(2,128)(2,1)S(1)}, bf16[80,9,2,128]{3,2,1,0:T(2,128)(2,1)S(1)}, bf16[80,9,2,128...) custom-call(s32[64]{0:T(128)S(1)} %copy-done.5, ...), custom_call_target="tpu_custom_call" | custom-call | flops 2211840 | bytes 4423680 | tf_op jit(solution)/shard_map/cut/pallas_call | solution.py:87
  6.0 2.5 %cut.7 = (bf16[80,9,2,128]{3,2,1,0:T(2,128)(2,1)S(1)}, bf16[80,9,2,128]{3,2,1,0:T(2,128)(2,1)S(1)}, bf16[80,9,2,128]{3,2,1,0:T(2,128)(2,1)S(1)}, bf16[80,9,2,128...) custom-call(s32[64]{0:T(128)S(1)} %copy-done.5, ...), custom_call_target="tpu_custom_call" | custom-call | flops 2211840 | bytes 4423680 | tf_op jit(solution)/shard_map/cut/pallas_call | solution.py:87
  8.5 2.8 %cut.8 = (bf16[80,9,2,128]{3,2,1,0:T(2,128)(2,1)S(1)}, bf16[80,9,2,128]{3,2,1,0:T(2,128)(2,1)S(1)}, bf16[80,9,2,128]{3,2,1,0:T(2,128)(2,1)S(1)}, bf16[80,9,2,128...) custom-call(s32[64]{0:T(128)S(1)} %copy-done.5, ...), custom_call_target="tpu_custom_call" | custom-call | flops 2949120 | bytes 5898240 | tf_op jit(solution)/shard_map/cut/pallas_call | solution.py:87
  11.3 3.0 %collective-permute-start.4 = (bf16[80,9,2,128]{3,2,1,0:T(2,128)(2,1)S(1)}, bf16[80,9,2,128]{3,2,1,0:T(2,128)(2,1)S(1)}, u32[]{:S(2)}, u32[]{:S(2)}) collective-permute-start(bf16[80,9,2,128]{3,2,1,0:T(2,128)(2,1)S(1)} %get-tuple-element.90.rest_0_), channel_id=1, source_target_pairs={{0,22},{1,23},{2,16},{3,17},{4,18},{5,19},{6,20},{7,21},{8,30},{9,... | collective-permute-start | bytes 1105928 | tf_op jit(solution)/shard_map/ppermute | solution.py:338
  15.8 2.8 %cut.9 = (bf16[80,9,2,128]{3,2,1,0:T(2,128)(2,1)S(1)}, bf16[80,9,2,128]{3,2,1,0:T(2,128)(2,1)S(1)}, bf16[80,9,2,128]{3,2,1,0:T(2,128)(2,1)S(1)}, bf16[80,9,2,128...) custom-call(s32[64]{0:T(128)S(1)} %copy-done.6, ...), custom_call_target="tpu_custom_call" | custom-call | flops 2949120 | bytes 5898240 | tf_op jit(solution)/shard_map/cut/pallas_call | solution.py:87
  18.6 3.0 %collective-permute-start.7 = (bf16[80,9,2,128]{3,2,1,0:T(2,128)(2,1)S(1)}, bf16[80,9,2,128]{3,2,1,0:T(2,128)(2,1)S(1)}, u32[]{:S(2)}, u32[]{:S(2)}) collective-permute-start(bf16[80,9,2,128]{3,2,1,0:T(2,128)(2,1)S(1)} %get-tuple-element.97), channel_id=1, source_target_pairs={{0,19},{1,18},{2,21},{3,20},{4,23},{5,22},{6,17},{7,16},{8,27},{9,... | collective-permute-start | bytes 1105928 | tf_op jit(solution)/shard_map/ppermute | solution.py:338
  22.6 3.1 %collective-permute-start.9 = (bf16[80,9,2,128]{3,2,1,0:T(2,128)(2,1)S(1)}, bf16[80,9,2,128]{3,2,1,0:T(2,128)(2,1)S(1)}, u32[]{:S(2)}, u32[]{:S(2)}) collective-permute-start(bf16[80,9,2,128]{3,2,1,0:T(2,128)(2,1)S(1)} %get-tuple-element.99), channel_id=1, source_target_pairs={{0,5},{1,4},{2,7},{3,6},{4,1},{5,0},{6,3},{7,2},{8,13},{9,12},{10,... | collective-permute-start | bytes 1105928 | tf_op jit(solution)/shard_map/ppermute | solution.py:338
  25.7 2.6 %collective-permute-start.10 = (bf16[80,9,2,128]{3,2,1,0:T(2,128)(2,1)S(1)}, bf16[80,9,2,128]{3,2,1,0:T(2,128)(2,1)S(1)}, u32[]{:S(2)}, u32[]{:S(2)}) collective-permute-start(bf16[80,9,2,128]{3,2,1,0:T(2,128)(2,1)S(1)} %get-tuple-element.100), channel_id=1, source_target_pairs={{0,16},{1,17},{2,18},{3,19},{4,20},{5,21},{6,22},{7,23},{8,24},{9,... | collective-permute-start | bytes 1105928 | tf_op jit(solution)/shard_map/ppermute | solution.py:338
  28.3 6.4 %collective-permute-done.6 = bf16[80,9,2,128]{3,2,1,0:T(2,128)(2,1)S(1)} collective-permute-done((bf16[80,9,2,128]{3,2,1,0:T(2,128)(2,1)S(1)}, bf16[80,9,2,128]{3,2,1,0:T(2,128)(2,1)S(1)}, u32[]{:S(2)}, u32[]{:S(2)}) %collective-permute-start.6) | collective-permute-done | bytes 368672 | tf_op jit(solution)/shard_map/ppermute | solution.py:338
  35.1 5.3 %collective-permute-done.7 = bf16[80,9,2,128]{3,2,1,0:T(2,128)(2,1)S(1)} collective-permute-done((bf16[80,9,2,128]{3,2,1,0:T(2,128)(2,1)S(1)}, bf16[80,9,2,128]{3,2,1,0:T(2,128)(2,1)S(1)}, u32[]{:S(2)}, u32[]{:S(2)}) %collective-permute-start.7) | collective-permute-done | bytes 368672 | tf_op jit(solution)/shard_map/ppermute | solution.py:338
  42.1 7.6 %collective-permute-start.13 = (bf16[80,9,2,128]{3,2,1,0:T(2,128)(2,1)S(1)}, bf16[80,9,2,128]{3,2,1,0:T(2,128)(2,1)S(1)}, u32[]{:S(2)}, u32[]{:S(2)}) collective-permute-start(bf16[80,9,2,128]{3,2,1,0:T(2,128)(2,1)S(1)} %get-tuple-element.103), channel_id=1, source_target_pairs={{0,7},{1,6},{2,1},{3,0},{4,3},{5,2},{6,5},{7,4},{8,15},{9,14},{10,... | collective-permute-start | bytes 1105928 | tf_op jit(solution)/shard_map/ppermute | solution.py:338
  49.7 8.9 %collective-permute-start.14 = (bf16[80,9,2,128]{3,2,1,0:T(2,128)(2,1)S(1)}, bf16[80,9,2,128]{3,2,1,0:T(2,128)(2,1)S(1)}, u32[]{:S(2)}, u32[]{:S(2)}) collective-permute-start(bf16[80,9,2,128]{3,2,1,0:T(2,128)(2,1)S(1)} %get-tuple-element.104), channel_id=1, source_target_pairs={{0,2},{1,3},{2,4},{3,5},{4,6},{5,7},{6,0},{7,1},{8,10},{9,11},{10,... | collective-permute-start | bytes 1105928 | tf_op jit(solution)/shard_map/ppermute | solution.py:338
  58.6 2.5 %collective-permute-start.16 = (bf16[80,9,2,128]{3,2,1,0:T(2,128)(2,1)S(1)}, bf16[80,9,2,128]{3,2,1,0:T(2,128)(2,1)S(1)}, u32[]{:S(2)}, u32[]{:S(2)}) collective-permute-start(bf16[80,9,2,128]{3,2,1,0:T(2,128)(2,1)S(1)} %get-tuple-element.106), channel_id=1, source_target_pairs={{0,24},{1,25},{2,26},{3,27},{4,28},{5,29},{6,30},{7,31},{8,0},{9,1... | collective-permute-start | bytes 1105928 | tf_op jit(solution)/shard_map/ppermute | solution.py:338
  62.6 5.0 %collective-permute-done.14 = bf16[80,9,2,128]{3,2,1,0:T(2,128)(2,1)S(1)} collective-permute-done((bf16[80,9,2,128]{3,2,1,0:T(2,128)(2,1)S(1)}, bf16[80,9,2,128]{3,2,1,0:T(2,128)(2,1)S(1)}, u32[]{:S(2)}, u32[]{:S(2)}) %collective-permute-start.14) | collective-permute-done | bytes 368672 | tf_op jit(solution)/shard_map/ppermute | solution.py:338
  67.6 7.0 %collective-permute-done.15 = bf16[80,9,2,128]{3,2,1,0:T(2,128)(2,1)S(1)} collective-permute-done((bf16[80,9,2,128]{3,2,1,0:T(2,128)(2,1)S(1)}, bf16[80,9,2,128]{3,2,1,0:T(2,128)(2,1)S(1)}, u32[]{:S(2)}, u32[]{:S(2)}) %collective-permute-start.15) | collective-permute-done | bytes 368672 | tf_op jit(solution)/shard_map/ppermute | solution.py:338
  74.6 3.1 %collective-permute-start.20 = (bf16[80,9,2,128]{3,2,1,0:T(2,128)(2,1)S(1)}, bf16[80,9,2,128]{3,2,1,0:T(2,128)(2,1)S(1)}, u32[]{:S(2)}, u32[]{:S(2)}) collective-permute-start(bf16[80,9,2,128]{3,2,1,0:T(2,128)(2,1)S(1)} %get-tuple-element.109), channel_id=1, source_target_pairs={{0,20},{1,21},{2,22},{3,23},{4,16},{5,17},{6,18},{7,19},{8,28},{9,... | collective-permute-start | bytes 1105928 | tf_op jit(solution)/shard_map/ppermute | solution.py:338
  79.9 4.3 %collective-permute-start.22 = (bf16[80,9,2,128]{3,2,1,0:T(2,128)(2,1)S(1)}, bf16[80,9,2,128]{3,2,1,0:T(2,128)(2,1)S(1)}, u32[]{:S(2)}, u32[]{:S(2)}) collective-permute-start(bf16[80,9,2,128]{3,2,1,0:T(2,128)(2,1)S(1)} %get-tuple-element.87.rest_0_), channel_id=1, source_target_pairs={{0,26},{1,27},{2,28},{3,29},{4,30},{5,31},{6,24},{7,25},{8,2},{9,3... | collective-permute-start | bytes 1105928 | tf_op jit(solution)/shard_map/ppermute | solution.py:338
  86.2 3.9 %collective-permute-done.20 = bf16[80,9,2,128]{3,2,1,0:T(2,128)(2,1)S(1)} collective-permute-done((bf16[80,9,2,128]{3,2,1,0:T(2,128)(2,1)S(1)}, bf16[80,9,2,128]{3,2,1,0:T(2,128)(2,1)S(1)}, u32[]{:S(2)}, u32[]{:S(2)}) %collective-permute-start.20) | collective-permute-done | bytes 368672 | tf_op jit(solution)/shard_map/ppermute | solution.py:338
  91.8 4.6 %collective-permute-done.21 = bf16[80,9,2,128]{3,2,1,0:T(2,128)(2,1)S(1)} collective-permute-done((bf16[80,9,2,128]{3,2,1,0:T(2,128)(2,1)S(1)}, bf16[80,9,2,128]{3,2,1,0:T(2,128)(2,1)S(1)}, u32[]{:S(2)}, u32[]{:S(2)}) %collective-permute-start.21) | collective-permute-done | bytes 368672 | tf_op jit(solution)/shard_map/ppermute | solution.py:338
  96.4 6.8 %collective-permute-start.26 = (bf16[80,9,2,128]{3,2,1,0:T(2,128)(2,1)S(1)}, bf16[80,9,2,128]{3,2,1,0:T(2,128)(2,1)S(1)}, u32[]{:S(2)}, u32[]{:S(2)}) collective-permute-start(bf16[80,9,2,128]{3,2,1,0:T(2,128)(2,1)S(1)} %get-tuple-element.113), channel_id=1, source_target_pairs={{0,30},{1,31},{2,24},{3,25},{4,26},{5,27},{6,28},{7,29},{8,6},{9,7... | collective-permute-start | bytes 1105928 | tf_op jit(solution)/shard_map/ppermute | solution.py:338
  103.2 2.9 %collective-permute-done.22 = bf16[80,9,2,128]{3,2,1,0:T(2,128)(2,1)S(1)} collective-permute-done((bf16[80,9,2,128]{3,2,1,0:T(2,128)(2,1)S(1)}, bf16[80,9,2,128]{3,2,1,0:T(2,128)(2,1)S(1)}, u32[]{:S(2)}, u32[]{:S(2)}) %collective-permute-start.22) | collective-permute-done | bytes 368672 | tf_op jit(solution)/shard_map/ppermute | solution.py:338
  106.1 2.3 %collective-permute-start.27 = (bf16[80,9,2,128]{3,2,1,0:T(2,128)(2,1)S(1)}, bf16[80,9,2,128]{3,2,1,0:T(2,128)(2,1)S(1)}, u32[]{:S(2)}, u32[]{:S(2)}) collective-permute-start(bf16[80,9,2,128]{3,2,1,0:T(2,128)(2,1)S(1)} %get-tuple-element.114), channel_id=1, source_target_pairs={{0,31},{1,30},{2,25},{3,24},{4,27},{5,26},{6,29},{7,28},{8,7},{9,6... | collective-permute-start | bytes 1105928 | tf_op jit(solution)/shard_map/ppermute | solution.py:338
  108.4 5.8 %collective-permute-done.23 = bf16[80,9,2,128]{3,2,1,0:T(2,128)(2,1)S(1)} collective-permute-done((bf16[80,9,2,128]{3,2,1,0:T(2,128)(2,1)S(1)}, bf16[80,9,2,128]{3,2,1,0:T(2,128)(2,1)S(1)}, u32[]{:S(2)}, u32[]{:S(2)}) %collective-permute-start.23) | collective-permute-done | bytes 368672 | tf_op jit(solution)/shard_map/ppermute | solution.py:338
  116.7 5.0 %collective-permute-done.26 = bf16[80,9,2,128]{3,2,1,0:T(2,128)(2,1)S(1)} collective-permute-done((bf16[80,9,2,128]{3,2,1,0:T(2,128)(2,1)S(1)}, bf16[80,9,2,128]{3,2,1,0:T(2,128)(2,1)S(1)}, u32[]{:S(2)}, u32[]{:S(2)}) %collective-permute-start.26) | collective-permute-done | bytes 368672 | tf_op jit(solution)/shard_map/ppermute | solution.py:338
  121.7 2.5 %collective-permute-start.5 = (bf16[80,9,2,128]{3,2,1,0:T(2,128)(2,1)S(1)}, bf16[80,9,2,128]{3,2,1,0:T(2,128)(2,1)S(1)}, u32[]{:S(2)}, u32[]{:S(2)}) collective-permute-start(bf16[80,9,2,128]{3,2,1,0:T(2,128)(2,1)S(1)} %get-tuple-element.95), channel_id=1, source_target_pairs={{0,23},{1,22},{2,17},{3,16},{4,19},{5,18},{6,21},{7,20},{8,31},{9,... | collective-permute-start | bytes 1105928 | tf_op jit(solution)/shard_map/ppermute | solution.py:338
  124.2 6.0 %collective-permute-done.27 = bf16[80,9,2,128]{3,2,1,0:T(2,128)(2,1)S(1)} collective-permute-done((bf16[80,9,2,128]{3,2,1,0:T(2,128)(2,1)S(1)}, bf16[80,9,2,128]{3,2,1,0:T(2,128)(2,1)S(1)}, u32[]{:S(2)}, u32[]{:S(2)}) %collective-permute-start.27) | collective-permute-done | bytes 368672 | tf_op jit(solution)/shard_map/ppermute | solution.py:338
  130.2 3.7 %collective-permute-start = (bf16[80,9,2,128]{3,2,1,0:T(2,128)(2,1)S(1)}, bf16[80,9,2,128]{3,2,1,0:T(2,128)(2,1)S(1)}, u32[]{:S(2)}, u32[]{:S(2)}) collective-permute-start(bf16[80,9,2,128]{3,2,1,0:T(2,128)(2,1)S(1)} %get-tuple-element.91), channel_id=1, source_target_pairs={{0,28},{1,29},{2,30},{3,31},{4,24},{5,25},{6,26},{7,27},{8,4},{9,5... | collective-permute-start | bytes 1105928 | tf_op jit(solution)/shard_map/ppermute | solution.py:338
  133.9 3.8 %collective-permute-start.2 = (bf16[80,9,2,128]{3,2,1,0:T(2,128)(2,1)S(1)}, bf16[80,9,2,128]{3,2,1,0:T(2,128)(2,1)S(1)}, u32[]{:S(2)}, u32[]{:S(2)}) collective-permute-start(bf16[80,9,2,128]{3,2,1,0:T(2,128)(2,1)S(1)} %get-tuple-element.93), channel_id=1, source_target_pairs={{0,12},{1,13},{2,14},{3,15},{4,8},{5,9},{6,10},{7,11},{8,20},{9,21... | collective-permute-start | bytes 1105928 | tf_op jit(solution)/shard_map/ppermute | solution.py:338
  169.9 3.7 %collective-permute-done.1 = bf16[80,9,2,128]{3,2,1,0:T(2,128)(2,1)S(1)} collective-permute-done((bf16[80,9,2,128]{3,2,1,0:T(2,128)(2,1)S(1)}, bf16[80,9,2,128]{3,2,1,0:T(2,128)(2,1)S(1)}, u32[]{:S(2)}, u32[]{:S(2)}) %collective-permute-start.1) | collective-permute-done | bytes 368672 | tf_op jit(solution)/shard_map/ppermute | solution.py:338
  174.9 4.1 %collective-permute-done.31.b = f32[32,256]{1,0:T(8,128)S(1)} collective-permute-done((f32[32,256]{1,0:T(8,128)S(1)}, f32[32,256]{1,0:T(8,128)S(1)}, u32[]{:S(2)}, u32[]{:S(2)}) %collective-permute-start.31) | collective-permute-done | bytes 32800 | tf_op jit(solution)/shard_map/ppermute | solution.py:347
  181.0 3.1 %pick.1 = (f32[2,18]{1,0:T(2,128)S(1)}, f32[2,2]{1,0:T(2,128)S(1)}) custom-call(s32[64]{0:T(128)S(1)} %copy-done.6, s32[2]{0:T(128)S(1)} %copy-done.8, s32[46,64]{1,0:T(8,128)S(1)} %copy-done.4, s32[46,576]{1,0:T(8,128)S(1)} %copy-done.2), custom_call_target="tpu_custom_call" | custom-call | tf_op jit(solution)/shard_map/pick/pallas_call | solution.py:292
  186.3 2.8 %serve.31 = (bf16[2,20736,128]{2,1,0:T(8,128)(2,1)}, bf16[2,2304,128]{2,1,0:T(8,128)(2,1)}, f32[32,256]{1,0:T(8,128)}) custom-call(bf16[168,144]{1,0:T(8,128)(2,1)S(1)} %copy-done, bf16[2,152,72]{2,1,0:T(8,128)(2,1)S(1)} %copy-done.1, bf16[1440,128]{1,0:T(8,128)(2,1)S(1)} %bitcast.53, ...), custom_call_target="tpu_custom_call", output_to_operand_aliasing={{0}: (4, {}), {1}: (5, {})} | custom-call | flops 123863040 | bytes 3145728 | tf_op jit(solution)/shard_map/serve/pallas_call | solution.py:199
  (77 shorter events, 55.4 us)
Async XLA Ops:
  11.3 14.4 %collective-permute-start.4 = (bf16[80,9,2,128]{3,2,1,0:T(2,128)(2,1)S(1)}, bf16[80,9,2,128]{3,2,1,0:T(2,128)(2,1)S(1)}, u32[]{:S(2)}, u32[]{:S(2)}) collective-permute-start(bf16[80,9,2,128]{3,2,1,0:T(2,128)(2,1)S(1)} %get-tuple-element.90.rest_0_), channel_id=1, source_target_pairs={{0,22},{1,23},{2,16},{3,17},{4,18},{5,19},{6,20},{7,21},{8,30},{9,... | collective-permute-start | bytes 1105928 | tf_op jit(solution)/shard_map/ppermute | solution.py:338
  14.3 20.4 %collective-permute-start.6 = (bf16[80,9,2,128]{3,2,1,0:T(2,128)(2,1)S(1)}, bf16[80,9,2,128]{3,2,1,0:T(2,128)(2,1)S(1)}, u32[]{:S(2)}, u32[]{:S(2)}) collective-permute-start(bf16[80,9,2,128]{3,2,1,0:T(2,128)(2,1)S(1)} %get-tuple-element.96), channel_id=1, source_target_pairs={{0,18},{1,19},{2,20},{3,21},{4,22},{5,23},{6,16},{7,17},{8,26},{9,... | collective-permute-start | bytes 1105928 | tf_op jit(solution)/shard_map/ppermute | solution.py:338
  18.6 21.7 %collective-permute-start.7 = (bf16[80,9,2,128]{3,2,1,0:T(2,128)(2,1)S(1)}, bf16[80,9,2,128]{3,2,1,0:T(2,128)(2,1)S(1)}, u32[]{:S(2)}, u32[]{:S(2)}) collective-permute-start(bf16[80,9,2,128]{3,2,1,0:T(2,128)(2,1)S(1)} %get-tuple-element.97), channel_id=1, source_target_pairs={{0,19},{1,18},{2,21},{3,20},{4,23},{5,22},{6,17},{7,16},{8,27},{9,... | collective-permute-start | bytes 1105928 | tf_op jit(solution)/shard_map/ppermute | solution.py:338
  21.6 20.5 %collective-permute-start.8 = (bf16[80,9,2,128]{3,2,1,0:T(2,128)(2,1)S(1)}, bf16[80,9,2,128]{3,2,1,0:T(2,128)(2,1)S(1)}, u32[]{:S(2)}, u32[]{:S(2)}) collective-permute-start(bf16[80,9,2,128]{3,2,1,0:T(2,128)(2,1)S(1)} %get-tuple-element.98), channel_id=1, source_target_pairs={{0,4},{1,5},{2,6},{3,7},{4,0},{5,1},{6,2},{7,3},{8,12},{9,13},{10,... | collective-permute-start | bytes 1105928 | tf_op jit(solution)/shard_map/ppermute | solution.py:338
  22.6 27.1 %collective-permute-start.9 = (bf16[80,9,2,128]{3,2,1,0:T(2,128)(2,1)S(1)}, bf16[80,9,2,128]{3,2,1,0:T(2,128)(2,1)S(1)}, u32[]{:S(2)}, u32[]{:S(2)}) collective-permute-start(bf16[80,9,2,128]{3,2,1,0:T(2,128)(2,1)S(1)} %get-tuple-element.99), channel_id=1, source_target_pairs={{0,5},{1,4},{2,7},{3,6},{4,1},{5,0},{6,3},{7,2},{8,13},{9,12},{10,... | collective-permute-start | bytes 1105928 | tf_op jit(solution)/shard_map/ppermute | solution.py:338
  25.7 32.9 %collective-permute-start.10 = (bf16[80,9,2,128]{3,2,1,0:T(2,128)(2,1)S(1)}, bf16[80,9,2,128]{3,2,1,0:T(2,128)(2,1)S(1)}, u32[]{:S(2)}, u32[]{:S(2)}) collective-permute-start(bf16[80,9,2,128]{3,2,1,0:T(2,128)(2,1)S(1)} %get-tuple-element.100), channel_id=1, source_target_pairs={{0,16},{1,17},{2,18},{3,19},{4,20},{5,21},{6,22},{7,23},{8,24},{9,... | collective-permute-start | bytes 1105928 | tf_op jit(solution)/shard_map/ppermute | solution.py:338
  34.7 23.9 %collective-permute-start.11 = (bf16[80,9,2,128]{3,2,1,0:T(2,128)(2,1)S(1)}, bf16[80,9,2,128]{3,2,1,0:T(2,128)(2,1)S(1)}, u32[]{:S(2)}, u32[]{:S(2)}) collective-permute-start(bf16[80,9,2,128]{3,2,1,0:T(2,128)(2,1)S(1)} %get-tuple-element.101), channel_id=1, source_target_pairs={{0,17},{1,16},{2,19},{3,18},{4,21},{5,20},{6,23},{7,22},{8,25},{9,... | collective-permute-start | bytes 1105928 | tf_op jit(solution)/shard_map/ppermute | solution.py:338
  40.3 20.8 %collective-permute-start.12 = (bf16[80,9,2,128]{3,2,1,0:T(2,128)(2,1)S(1)}, bf16[80,9,2,128]{3,2,1,0:T(2,128)(2,1)S(1)}, u32[]{:S(2)}, u32[]{:S(2)}) collective-permute-start(bf16[80,9,2,128]{3,2,1,0:T(2,128)(2,1)S(1)} %get-tuple-element.102), channel_id=1, source_target_pairs={{0,6},{1,7},{2,0},{3,1},{4,2},{5,3},{6,4},{7,5},{8,14},{9,15},{10,... | collective-permute-start | bytes 1105928 | tf_op jit(solution)/shard_map/ppermute | solution.py:338
  42.1 19.1 %collective-permute-start.13 = (bf16[80,9,2,128]{3,2,1,0:T(2,128)(2,1)S(1)}, bf16[80,9,2,128]{3,2,1,0:T(2,128)(2,1)S(1)}, u32[]{:S(2)}, u32[]{:S(2)}) collective-permute-start(bf16[80,9,2,128]{3,2,1,0:T(2,128)(2,1)S(1)} %get-tuple-element.103), channel_id=1, source_target_pairs={{0,7},{1,6},{2,1},{3,0},{4,3},{5,2},{6,5},{7,4},{8,15},{9,14},{10,... | collective-permute-start | bytes 1105928 | tf_op jit(solution)/shard_map/ppermute | solution.py:338
  49.7 17.9 %collective-permute-start.14 = (bf16[80,9,2,128]{3,2,1,0:T(2,128)(2,1)S(1)}, bf16[80,9,2,128]{3,2,1,0:T(2,128)(2,1)S(1)}, u32[]{:S(2)}, u32[]{:S(2)}) collective-permute-start(bf16[80,9,2,128]{3,2,1,0:T(2,128)(2,1)S(1)} %get-tuple-element.104), channel_id=1, source_target_pairs={{0,2},{1,3},{2,4},{3,5},{4,6},{5,7},{6,0},{7,1},{8,10},{9,11},{10,... | collective-permute-start | bytes 1105928 | tf_op jit(solution)/shard_map/ppermute | solution.py:338
  58.6 16.0 %collective-permute-start.15 = (bf16[80,9,2,128]{3,2,1,0:T(2,128)(2,1)S(1)}, bf16[80,9,2,128]{3,2,1,0:T(2,128)(2,1)S(1)}, u32[]{:S(2)}, u32[]{:S(2)}) collective-permute-start(bf16[80,9,2,128]{3,2,1,0:T(2,128)(2,1)S(1)} %get-tuple-element.105), channel_id=1, source_target_pairs={{0,3},{1,2},{2,5},{3,4},{4,7},{5,6},{6,1},{7,0},{8,11},{9,10},{10,... | collective-permute-start | bytes 1105928 | tf_op jit(solution)/shard_map/ppermute | solution.py:338
  58.6 19.1 %collective-permute-start.16 = (bf16[80,9,2,128]{3,2,1,0:T(2,128)(2,1)S(1)}, bf16[80,9,2,128]{3,2,1,0:T(2,128)(2,1)S(1)}, u32[]{:S(2)}, u32[]{:S(2)}) collective-permute-start(bf16[80,9,2,128]{3,2,1,0:T(2,128)(2,1)S(1)} %get-tuple-element.106), channel_id=1, source_target_pairs={{0,24},{1,25},{2,26},{3,27},{4,28},{5,29},{6,30},{7,31},{8,0},{9,1... | collective-permute-start | bytes 1105928 | tf_op jit(solution)/shard_map/ppermute | solution.py:338
  61.2 18.8 %collective-permute-start.17 = (bf16[80,9,2,128]{3,2,1,0:T(2,128)(2,1)S(1)}, bf16[80,9,2,128]{3,2,1,0:T(2,128)(2,1)S(1)}, u32[]{:S(2)}, u32[]{:S(2)}) collective-permute-start(bf16[80,9,2,128]{3,2,1,0:T(2,128)(2,1)S(1)} %get-tuple-element.89.rest_0_), channel_id=1, source_target_pairs={{0,25},{1,24},{2,27},{3,26},{4,29},{5,28},{6,31},{7,30},{8,1},{9,0... | collective-permute-start | bytes 1105928 | tf_op jit(solution)/shard_map/ppermute | solution.py:338
  61.2 23.1 %collective-permute-start.18 = (bf16[80,9,2,128]{3,2,1,0:T(2,128)(2,1)S(1)}, bf16[80,9,2,128]{3,2,1,0:T(2,128)(2,1)S(1)}, u32[]{:S(2)}, u32[]{:S(2)}) collective-permute-start(bf16[80,9,2,128]{3,2,1,0:T(2,128)(2,1)S(1)} %get-tuple-element.107), channel_id=1, source_target_pairs={{0,8},{1,9},{2,10},{3,11},{4,12},{5,13},{6,14},{7,15},{8,16},{9,17... | collective-permute-start | bytes 1105928 | tf_op jit(solution)/shard_map/ppermute | solution.py:338
  67.6 16.7 %collective-permute-start.19 = (bf16[80,9,2,128]{3,2,1,0:T(2,128)(2,1)S(1)}, bf16[80,9,2,128]{3,2,1,0:T(2,128)(2,1)S(1)}, u32[]{:S(2)}, u32[]{:S(2)}) collective-permute-start(bf16[80,9,2,128]{3,2,1,0:T(2,128)(2,1)S(1)} %get-tuple-element.108), channel_id=1, source_target_pairs={{0,9},{1,8},{2,11},{3,10},{4,13},{5,12},{6,15},{7,14},{8,17},{9,16... | collective-permute-start | bytes 1105928 | tf_op jit(solution)/shard_map/ppermute | solution.py:338
  74.6 15.5 %collective-permute-start.20 = (bf16[80,9,2,128]{3,2,1,0:T(2,128)(2,1)S(1)}, bf16[80,9,2,128]{3,2,1,0:T(2,128)(2,1)S(1)}, u32[]{:S(2)}, u32[]{:S(2)}) collective-permute-start(bf16[80,9,2,128]{3,2,1,0:T(2,128)(2,1)S(1)} %get-tuple-element.109), channel_id=1, source_target_pairs={{0,20},{1,21},{2,22},{3,23},{4,16},{5,17},{6,18},{7,19},{8,28},{9,... | collective-permute-start | bytes 1105928 | tf_op jit(solution)/shard_map/ppermute | solution.py:338
  77.7 18.7 %collective-permute-start.21 = (bf16[80,9,2,128]{3,2,1,0:T(2,128)(2,1)S(1)}, bf16[80,9,2,128]{3,2,1,0:T(2,128)(2,1)S(1)}, u32[]{:S(2)}, u32[]{:S(2)}) collective-permute-start(bf16[80,9,2,128]{3,2,1,0:T(2,128)(2,1)S(1)} %get-tuple-element.88.rest_0_), channel_id=1, source_target_pairs={{0,21},{1,20},{2,23},{3,22},{4,17},{5,16},{6,19},{7,18},{8,29},{9,... | collective-permute-start | bytes 1105928 | tf_op jit(solution)/shard_map/ppermute | solution.py:338
  79.9 26.2 %collective-permute-start.22 = (bf16[80,9,2,128]{3,2,1,0:T(2,128)(2,1)S(1)}, bf16[80,9,2,128]{3,2,1,0:T(2,128)(2,1)S(1)}, u32[]{:S(2)}, u32[]{:S(2)}) collective-permute-start(bf16[80,9,2,128]{3,2,1,0:T(2,128)(2,1)S(1)} %get-tuple-element.87.rest_0_), channel_id=1, source_target_pairs={{0,26},{1,27},{2,28},{3,29},{4,30},{5,31},{6,24},{7,25},{8,2},{9,3... | collective-permute-start | bytes 1105928 | tf_op jit(solution)/shard_map/ppermute | solution.py:338
  84.3 30.0 %collective-permute-start.23 = (bf16[80,9,2,128]{3,2,1,0:T(2,128)(2,1)S(1)}, bf16[80,9,2,128]{3,2,1,0:T(2,128)(2,1)S(1)}, u32[]{:S(2)}, u32[]{:S(2)}) collective-permute-start(bf16[80,9,2,128]{3,2,1,0:T(2,128)(2,1)S(1)} %get-tuple-element.110), channel_id=1, source_target_pairs={{0,27},{1,26},{2,29},{3,28},{4,31},{5,30},{6,25},{7,24},{8,3},{9,2... | collective-permute-start | bytes 1105928 | tf_op jit(solution)/shard_map/ppermute | solution.py:338
  84.3 31.9 %collective-permute-start.24 = (bf16[80,9,2,128]{3,2,1,0:T(2,128)(2,1)S(1)}, bf16[80,9,2,128]{3,2,1,0:T(2,128)(2,1)S(1)}, u32[]{:S(2)}, u32[]{:S(2)}) collective-permute-start(bf16[80,9,2,128]{3,2,1,0:T(2,128)(2,1)S(1)} %get-tuple-element.111), channel_id=1, source_target_pairs={{0,14},{1,15},{2,8},{3,9},{4,10},{5,11},{6,12},{7,13},{8,22},{9,23... | collective-permute-start | bytes 1105928 | tf_op jit(solution)/shard_map/ppermute | solution.py:338
  90.1 26.1 %collective-permute-start.25 = (bf16[80,9,2,128]{3,2,1,0:T(2,128)(2,1)S(1)}, bf16[80,9,2,128]{3,2,1,0:T(2,128)(2,1)S(1)}, u32[]{:S(2)}, u32[]{:S(2)}) collective-permute-start(bf16[80,9,2,128]{3,2,1,0:T(2,128)(2,1)S(1)} %get-tuple-element.112), channel_id=1, source_target_pairs={{0,15},{1,14},{2,9},{3,8},{4,11},{5,10},{6,13},{7,12},{8,23},{9,22... | collective-permute-start | bytes 1105928 | tf_op jit(solution)/shard_map/ppermute | solution.py:338
  96.4 25.3 %collective-permute-start.26 = (bf16[80,9,2,128]{3,2,1,0:T(2,128)(2,1)S(1)}, bf16[80,9,2,128]{3,2,1,0:T(2,128)(2,1)S(1)}, u32[]{:S(2)}, u32[]{:S(2)}) collective-permute-start(bf16[80,9,2,128]{3,2,1,0:T(2,128)(2,1)S(1)} %get-tuple-element.113), channel_id=1, source_target_pairs={{0,30},{1,31},{2,24},{3,25},{4,26},{5,27},{6,28},{7,29},{8,6},{9,7... | collective-permute-start | bytes 1105928 | tf_op jit(solution)/shard_map/ppermute | solution.py:338
  106.1 24.1 %collective-permute-start.27 = (bf16[80,9,2,128]{3,2,1,0:T(2,128)(2,1)S(1)}, bf16[80,9,2,128]{3,2,1,0:T(2,128)(2,1)S(1)}, u32[]{:S(2)}, u32[]{:S(2)}) collective-permute-start(bf16[80,9,2,128]{3,2,1,0:T(2,128)(2,1)S(1)} %get-tuple-element.114), channel_id=1, source_target_pairs={{0,31},{1,30},{2,25},{3,24},{4,27},{5,26},{6,29},{7,28},{8,7},{9,6... | collective-permute-start | bytes 1105928 | tf_op jit(solution)/shard_map/ppermute | solution.py:338
  114.3 19.6 %collective-permute-start.28 = (bf16[80,9,2,128]{3,2,1,0:T(2,128)(2,1)S(1)}, bf16[80,9,2,128]{3,2,1,0:T(2,128)(2,1)S(1)}, u32[]{:S(2)}, u32[]{:S(2)}) collective-permute-start(bf16[80,9,2,128]{3,2,1,0:T(2,128)(2,1)S(1)} %get-tuple-element.115), channel_id=1, source_target_pairs={{0,10},{1,11},{2,12},{3,13},{4,14},{5,15},{6,8},{7,9},{8,18},{9,19... | collective-permute-start | bytes 1105928 | tf_op jit(solution)/shard_map/ppermute | solution.py:338
  116.2 17.7 %collective-permute-start.29 = (bf16[80,9,2,128]{3,2,1,0:T(2,128)(2,1)S(1)}, bf16[80,9,2,128]{3,2,1,0:T(2,128)(2,1)S(1)}, u32[]{:S(2)}, u32[]{:S(2)}) collective-permute-start(bf16[80,9,2,128]{3,2,1,0:T(2,128)(2,1)S(1)} %get-tuple-element.116), channel_id=1, source_target_pairs={{0,11},{1,10},{2,13},{3,12},{4,15},{5,14},{6,9},{7,8},{8,19},{9,18... | collective-permute-start | bytes 1105928 | tf_op jit(solution)/shard_map/ppermute | solution.py:338
  116.2 21.5 %collective-permute-start.30 = (bf16[80,9,2,128]{3,2,1,0:T(2,128)(2,1)S(1)}, bf16[80,9,2,128]{3,2,1,0:T(2,128)(2,1)S(1)}, u32[]{:S(2)}, u32[]{:S(2)}) collective-permute-start(bf16[80,9,2,128]{3,2,1,0:T(2,128)(2,1)S(1)} %get-tuple-element.118), channel_id=1, source_target_pairs={{0,1},{1,0},{2,3},{3,2},{4,5},{5,4},{6,7},{7,6},{8,9},{9,8},{10,11... | collective-permute-start | bytes 1105928 | tf_op jit(solution)/shard_map/ppermute | solution.py:338
  121.7 46.0 %collective-permute-start.5 = (bf16[80,9,2,128]{3,2,1,0:T(2,128)(2,1)S(1)}, bf16[80,9,2,128]{3,2,1,0:T(2,128)(2,1)S(1)}, u32[]{:S(2)}, u32[]{:S(2)}) collective-permute-start(bf16[80,9,2,128]{3,2,1,0:T(2,128)(2,1)S(1)} %get-tuple-element.95), channel_id=1, source_target_pairs={{0,23},{1,22},{2,17},{3,16},{4,19},{5,18},{6,21},{7,20},{8,31},{9,... | collective-permute-start | bytes 1105928 | tf_op jit(solution)/shard_map/ppermute | solution.py:338
  130.2 39.7 %collective-permute-start = (bf16[80,9,2,128]{3,2,1,0:T(2,128)(2,1)S(1)}, bf16[80,9,2,128]{3,2,1,0:T(2,128)(2,1)S(1)}, u32[]{:S(2)}, u32[]{:S(2)}) collective-permute-start(bf16[80,9,2,128]{3,2,1,0:T(2,128)(2,1)S(1)} %get-tuple-element.91), channel_id=1, source_target_pairs={{0,28},{1,29},{2,30},{3,31},{4,24},{5,25},{6,26},{7,27},{8,4},{9,5... | collective-permute-start | bytes 1105928 | tf_op jit(solution)/shard_map/ppermute | solution.py:338
  133.9 39.7 %collective-permute-start.1 = (bf16[80,9,2,128]{3,2,1,0:T(2,128)(2,1)S(1)}, bf16[80,9,2,128]{3,2,1,0:T(2,128)(2,1)S(1)}, u32[]{:S(2)}, u32[]{:S(2)}) collective-permute-start(bf16[80,9,2,128]{3,2,1,0:T(2,128)(2,1)S(1)} %get-tuple-element.92), channel_id=1, source_target_pairs={{0,29},{1,28},{2,31},{3,30},{4,25},{5,24},{6,27},{7,26},{8,5},{9,4... | collective-permute-start | bytes 1105928 | tf_op jit(solution)/shard_map/ppermute | solution.py:338
  133.9 39.7 %collective-permute-start.2 = (bf16[80,9,2,128]{3,2,1,0:T(2,128)(2,1)S(1)}, bf16[80,9,2,128]{3,2,1,0:T(2,128)(2,1)S(1)}, u32[]{:S(2)}, u32[]{:S(2)}) collective-permute-start(bf16[80,9,2,128]{3,2,1,0:T(2,128)(2,1)S(1)} %get-tuple-element.93), channel_id=1, source_target_pairs={{0,12},{1,13},{2,14},{3,15},{4,8},{5,9},{6,10},{7,11},{8,20},{9,21... | collective-permute-start | bytes 1105928 | tf_op jit(solution)/shard_map/ppermute | solution.py:338
  137.7 36.6 %collective-permute-start.3 = (bf16[80,9,2,128]{3,2,1,0:T(2,128)(2,1)S(1)}, bf16[80,9,2,128]{3,2,1,0:T(2,128)(2,1)S(1)}, u32[]{:S(2)}, u32[]{:S(2)}) collective-permute-start(bf16[80,9,2,128]{3,2,1,0:T(2,128)(2,1)S(1)} %get-tuple-element.94), channel_id=1, source_target_pairs={{0,13},{1,12},{2,15},{3,14},{4,9},{5,8},{6,11},{7,10},{8,21},{9,20... | collective-permute-start | bytes 1105928 | tf_op jit(solution)/shard_map/ppermute | solution.py:338
  179.1 10.1 %collective-permute-start.32 = (f32[32,256]{1,0:T(8,128)S(1)}, f32[32,256]{1,0:T(8,128)S(1)}, u32[]{:S(2)}, u32[]{:S(2)}) collective-permute-start(f32[32,256]{1,0:T(8,128)S(1)} %merge.1.a), channel_id=1, source_target_pairs={{0,96},{96,0},{32,64},{64,32},{1,97},{97,1},{33,65},{65,33},{2,98}... | collective-permute-start | bytes 98312 | tf_op jit(solution)/shard_map/ppermute | solution.py:350
  (10 other events, 339.6 us)
